TPU v7x, 128 devices: a whole 4x4x4 slice. The times are simulated.
128 devices in a mesh: table: 64 (over x, y, z), mp: 2 (over core).
Axes of the slice: x: 4, y: 4, z: 4, core: 2. Of those that a mesh axis runs over, the one named last changes fastest.
Arguments:
- hash_tables: bfloat16 [2, 65536, 4096], P(None, 'table', 'mp'), may hold values from -6 to 6
- byte_table: bfloat16 [256, 4096], P(None, 'mp'), may hold values from -6 to 6
- byte_ids: int32 [16384], P('table'), may hold values from 0 to 255
- hash_owner: int32 [2, 16384, 1], P(None, 'table'), may hold values from 0 to 63; in each aligned block of 256 rows (0 to 255, 256 to 511, ..., all dimensions but the last counted through in order) at most 8 rows name the same one
- hash_offset: int32 [2, 16384], P(None, 'table'), may hold values from 0 to 1023
- gain: float32 [4096], replicated, may hold values from 0.25 to 1.75
- proj_weight: bfloat16 [4096, 4096], P('table', 'mp'), may hold values from -0.09375 to 0.09375
- cotangent: bfloat16 [16384, 4096], P('table', 'mp'), may hold values from -6 to 6
Outputs:
- projected: bfloat16 [16384, 4096], P('table', 'mp')
- table_grads: bfloat16 [2, 65536, 4096], P(None, 'table', 'mp')
Inputs may be any that keep to these rules, and one draw needn't show every extreme that they name: `hash_owner`: within the 256 bytes of one device and one table, no owner is named more than 8 times, a bound that some of these blocks reach.
All inputs are finite; a program needn't handle non-finite values.
Results may differ from a plain program's by a relative error of at most 0.0058.
Values may be sent and summed in bfloat16 or wider, within the bound.
No kernel may reach another device: no remote copies, remote signals or barrier semaphores. Data moves between devices by JAX's collectives and lax.ppermute only.
A program may use at most 128 MiB of HBM per device.

v0:
```python
import functools
import jax
import jax.numpy as jnp
from jax import lax
from jax.experimental import pallas as pl
from jax.experimental.pallas import tpu as pltpu
from jax.sharding import PartitionSpec as P

eps = 1e-05
f32, bf16, i32 = jnp.float32, jnp.bfloat16, jnp.int32
LANES = 128


def iota(shape, dim):
    return lax.broadcasted_iota(i32, shape, dim)


def dot(a, b, ca, cb):
    return lax.dot_general(a, b, (((ca,), (cb,)), ((), ())), preferred_element_type=f32)


def route_body(owner_ref, offset_ref, wanted_ref, slot_ref, *, groups, cap):
    ngram, tokens = owner_ref.shape
    earlier = (iota((tokens, tokens), 0) < iota((tokens, tokens), 1)).astype(f32).astype(bf16)
    lane = iota((groups, LANES), 1)
    wanted = jnp.full((groups, LANES), -1, i32)
    for k in range(ngram):
        owner = owner_ref[k : k + 1, :]
        offset = offset_ref[k : k + 1, :]
        mine = jnp.broadcast_to(owner, (groups, tokens)) == iota((groups, tokens), 0)
        before = dot(mine.astype(f32).astype(bf16), earlier, 1, 0).astype(i32)
        rank = jnp.sum(jnp.where(mine, before, 0), axis=0, keepdims=True)
        slot_ref[k : k + 1, :] = owner * (ngram * cap) + k * cap + rank
        for r in range(cap):
            hit = jnp.where(mine & (before == r), offset + 1, 0)
            value = jnp.sum(hit, axis=1, keepdims=True) - 1
            wanted = jnp.where(lane == k * cap + r, value, wanted)
    wanted_ref[...] = wanted


def route(owner, offset, groups, cap):
    ngram, tokens = owner.shape
    return pl.pallas_call(
        functools.partial(route_body, groups=groups, cap=cap),
        out_shape=(
            jax.ShapeDtypeStruct((groups, LANES), i32),
            jax.ShapeDtypeStruct((ngram, tokens), i32),
        ),
        name="route",
    )(owner, offset)


def row_picks(asked, k, cap, rows):
    groups = asked.shape[0]
    total = groups * cap
    spread = (iota((total, groups), 0) // cap == iota((total, groups), 1)).astype(f32).astype(bf16)
    code = asked + 1
    high = (code >> 5).astype(f32).astype(bf16)
    low = (code & 31).astype(f32).astype(bf16)
    codes = dot(spread, high, 1, 0) * 32.0 + dot(spread, low, 1, 0)
    place = iota((total, LANES), 1) == k * cap + iota((total, LANES), 0) % cap
    column = jnp.sum(jnp.where(place, codes, 0.0), axis=1, keepdims=True).astype(i32) - 1
    return (column == iota((total, rows), 1)).astype(f32).astype(bf16)


def lookup_body(asked_ref, table_ref, out_ref, picks_ref, *, cap):
    k = pl.program_id(0)
    rows = table_ref.shape[1]

    @pl.when(pl.program_id(1) == 0)
    def _():
        picks_ref[...] = row_picks(asked_ref[...], k, cap, rows)

    out = dot(picks_ref[...], table_ref[0], 1, 0).astype(bf16)
    out_ref[...] = out.reshape(out_ref.shape)


def lookup(asked, tables, cap, block):
    groups = asked.shape[0]
    ngram, rows, width = tables.shape
    return pl.pallas_call(
        functools.partial(lookup_body, cap=cap),
        grid=(ngram, width // block),
        in_specs=[
            pl.BlockSpec((groups, LANES), lambda k, j: (0, 0)),
            pl.BlockSpec((1, rows, block), lambda k, j: (k, 0, j)),
        ],
        out_specs=pl.BlockSpec((groups, 1, cap, block), lambda k, j: (0, k, 0, j)),
        out_shape=jax.ShapeDtypeStruct((groups, ngram, cap, width), bf16),
        scratch_shapes=[pltpu.VMEM((groups * cap, rows), bf16)],
        name="lookup",
    )(asked, tables)


def slot_picks(slot, slots):
    ngram, tokens = slot.shape
    place = iota((slots, tokens), 0)
    hit = place == slot[0:1, :]
    for k in range(1, ngram):
        hit = hit | (place == slot[k : k + 1, :])
    return hit.astype(f32).astype(bf16)


def combine_body(slot_ref, ids_ref, fetched_ref, bytes_ref, out_ref, square_ref, picks_ref, codes_ref):
    slots, tokens = picks_ref.shape

    @pl.when(pl.program_id(0) == 0)
    def _():
        picks_ref[...] = slot_picks(slot_ref[...], slots)
        vocab = codes_ref.shape[0]
        codes_ref[...] = (iota((vocab, tokens), 0) == ids_ref[...]).astype(f32).astype(bf16)
        square_ref[...] = jnp.zeros(square_ref.shape, f32)

    block = out_ref.shape[1]
    fetched = fetched_ref[...].reshape(slots, block)
    summed = dot(picks_ref[...], fetched, 0, 0) + dot(codes_ref[...], bytes_ref[...], 0, 0)
    embedded = summed.astype(bf16)
    out_ref[...] = embedded
    values = embedded.astype(f32)
    square_ref[...] += jnp.sum(values * values, axis=1, keepdims=True)


def combine(slot, ids, fetched, byte_table, block):
    groups, ngram, cap, width = fetched.shape
    tokens = slot.shape[1]
    vocab = byte_table.shape[0]
    slots = groups * ngram * cap
    return pl.pallas_call(
        combine_body,
        grid=(width // block,),
        in_specs=[
            pl.BlockSpec((ngram, tokens), lambda j: (0, 0)),
            pl.BlockSpec((1, tokens), lambda j: (0, 0)),
            pl.BlockSpec((groups, ngram, cap, block), lambda j: (0, 0, 0, j)),
            pl.BlockSpec((vocab, block), lambda j: (0, j)),
        ],
        out_specs=(
            pl.BlockSpec((tokens, block), lambda j: (0, j)),
            pl.BlockSpec((tokens, 1), lambda j: (0, 0)),
        ),
        out_shape=(
            jax.ShapeDtypeStruct((tokens, width), bf16),
            jax.ShapeDtypeStruct((tokens, 1), f32),
        ),
        scratch_shapes=[pltpu.VMEM((slots, tokens), bf16), pltpu.VMEM((vocab, tokens), bf16)],
        name="combine",
    )(slot, ids.reshape(1, tokens), fetched, byte_table)


def dispatch_body(slot_ref, scaled_ref, embedded_ref, scale_ref, inner_ref, out_ref, picks_ref):
    slots, tokens = picks_ref.shape

    @pl.when(pl.program_id(0) == 0)
    def _():
        picks_ref[...] = slot_picks(slot_ref[...], slots)

    scale = scale_ref[...]
    values = embedded_ref[...].astype(f32)
    dembed = scale * scaled_ref[...] - values * (scale * scale * scale * inner_ref[...])
    out = dot(picks_ref[...], dembed.astype(bf16), 1, 0).astype(bf16)
    out_ref[...] = out.reshape(out_ref.shape)


def dispatch(slot, scaled, embedded, scale, inner, groups, cap, block):
    ngram, tokens = slot.shape
    width = embedded.shape[1]
    slots = groups * ngram * cap
    return pl.pallas_call(
        dispatch_body,
        grid=(width // block,),
        in_specs=[
            pl.BlockSpec((ngram, tokens), lambda j: (0, 0)),
            pl.BlockSpec((tokens, block), lambda j: (0, j)),
            pl.BlockSpec((tokens, block), lambda j: (0, j)),
            pl.BlockSpec((tokens, 1), lambda j: (0, 0)),
            pl.BlockSpec((tokens, 1), lambda j: (0, 0)),
        ],
        out_specs=pl.BlockSpec((groups, ngram, cap, block), lambda j: (0, 0, 0, j)),
        out_shape=jax.ShapeDtypeStruct((groups, ngram, cap, width), bf16),
        scratch_shapes=[pltpu.VMEM((slots, tokens), bf16)],
        name="dispatch",
    )(slot, scaled, embedded, scale, inner)


def accumulate_body(asked_ref, arrived_ref, out_ref, picks_ref, *, cap):
    k = pl.program_id(0)
    rows = out_ref.shape[1]
    groups = asked_ref.shape[0]

    @pl.when(pl.program_id(1) == 0)
    def _():
        picks_ref[...] = row_picks(asked_ref[...], k, cap, rows)

    arrived = arrived_ref[...].reshape(groups * cap, arrived_ref.shape[-1])
    out_ref[0] = dot(picks_ref[...], arrived, 0, 0).astype(bf16)


def accumulate(asked, arrived, rows, block):
    groups, ngram, cap, width = arrived.shape
    return pl.pallas_call(
        functools.partial(accumulate_body, cap=cap),
        grid=(ngram, width // block),
        in_specs=[
            pl.BlockSpec((groups, LANES), lambda k, j: (0, 0)),
            pl.BlockSpec((groups, 1, cap, block), lambda k, j: (0, k, 0, j)),
        ],
        out_specs=pl.BlockSpec((1, rows, block), lambda k, j: (k, 0, j)),
        out_shape=jax.ShapeDtypeStruct((ngram, rows, width), bf16),
        scratch_shapes=[pltpu.VMEM((groups * cap, rows), bf16)],
        name="accumulate",
    )(asked, arrived)


def exchange(array, axis):
    return lax.all_to_all(array, axis, split_axis=0, concat_axis=0, tiled=True)


def swapped(array):
    return lax.ppermute(array, "mp", [(0, 1), (1, 0)])


def on_device(
    hash_tables, byte_table, byte_ids, hash_owner, hash_offset, gain, proj_weight, cotangent
):
    groups = lax.axis_size("table")
    half = lax.axis_index("mp")
    ngram, rows, width = hash_tables.shape
    tokens = byte_ids.shape[0]
    full_width = gain.shape[0]
    cap = 2 * tokens // groups
    block = 512

    weight = lax.all_gather(proj_weight, "table", axis=0, tiled=True)
    wanted, slot = route(hash_owner[:, :, 0], hash_offset, groups, cap)
    asked = exchange(wanted.reshape(groups, 1, LANES), "table").reshape(groups, LANES)
    looked = lookup(asked, hash_tables, cap, block)
    fetched = exchange(looked, "table")
    embedded, square = combine(slot, byte_ids, fetched, byte_table, block)

    partial = dot(cotangent, weight, 1, 1)
    low, high = partial[:, :width], partial[:, width:]
    given = jnp.where(half == 0, high, low).astype(bf16)
    kept = jnp.where(half == 0, low, high)
    gain_half = lax.dynamic_slice_in_dim(gain, half * width, width)
    scaled = (kept + swapped(given).astype(f32)) * gain_half[None, :]
    inner = jnp.sum(embedded.astype(f32) * scaled, axis=1)
    sums = jnp.stack([square[:, 0], inner])
    sums = sums + swapped(sums)
    scale = lax.rsqrt(sums[0] / full_width + eps)[:, None]
    inner = (sums[1] / full_width)[:, None]
    sends = dispatch(slot, scaled, embedded, scale, inner, groups, cap, block)
    arrived = exchange(sends, "table")

    other = swapped(embedded)
    whole = jnp.where(
        half == 0,
        jnp.concatenate([embedded, other], axis=1),
        jnp.concatenate([other, embedded], axis=1),
    )
    normed = (whole.astype(f32) * scale * gain[None, :]).astype(bf16)
    projected = dot(normed, weight, 1, 0).astype(bf16)
    table_grads = accumulate(asked, arrived, rows, block)
    return (projected, table_grads)


def solution(mesh):
    return jax.shard_map(
        on_device,
        mesh=mesh,
        in_specs=(
            P(None, "table", "mp"),
            P(None, "mp"),
            P("table"),
            P(None, "table", None),
            P(None, "table"),
            P(),
            P("table", "mp"),
            P("table", "mp"),
        ),
        out_specs=(P("table", "mp"), P(None, "table", "mp")),
        check_vma=False,
    )
```

profile of v0, /device:TPU:2, one launch (start us, length us, event | category | flops | bytes accessed | tf_op | source)
XLA Modules:
  0.0 282.6 jit_solution(14384904402849022846)
XLA Ops:
  7.2 0.0 copy-start
  7.2 0.0 all-gather.2.cloned.1.call-start
  7.2 0.7 all-gather.2.cloned.1.call-update
  7.9 1.3 copy.17
  9.2 1.8 route.1
  11.0 20.1 %all_to_all.15 = s32[64,1,128]{2,1,0:T(1,128)} all-to-all(s32[64,1,128]{2,1,0:T(1,128)} %bitcast.19), channel_id=1, replica_groups=mesh['table'=64,'mp'=2] {'table'}, dimensions={0} | all-to-all | bytes 65536 | tf_op jit(solution)/shard_map/all_to_all | solution.py:215
  31.1 10.8 %lookup.1 = bf16[64,2,8,2048]{3,2,1,0:T(8,128)(2,1)} custom-call(s32[64,128]{1,0:T(8,128)} %bitcast.17, bf16[2,1024,2048]{2,1,0:T(8,128)(2,1)} %table_ref.1), custom_call_target="tpu_custom_call" | custom-call | tf_op jit(solution)/shard_map/lookup/pallas_call | solution.py:81
  42.0 6.7 %all-to-all-start.1 = ((bf16[64,2,8,2048]{3,2,1,0:T(8,128)(2,1)}), bf16[64,2,8,2048]{3,2,1,0:T(8,128)(2,1)}, u32[]{:S(2)}, u32[]{:S(2)}) async-start(bf16[64,2,8,2048]{3,2,1,0:T(8,128)(2,1)} %lookup.1), calls=%async_computation.1 | async-start | bytes 8388608 | tf_op jit(solution)/shard_map/all_to_all | solution.py:215
  48.7 117.1 %all-gather.2.cloned.1.call-done = bf16[4096,2048]{1,0:T(8,128)(2,1)} async-done(((bf16[64,2048]{1,0:T(8,128)(2,1)}), bf16[4096,2048]{1,0:T(8,128)(2,1)}) %all-gather.2.cloned.1.call-update) | async-done | bytes 16777232 | tf_op jit(solution)/shard_map/all_gather | solution.py:233
  165.8 0.0 copy-done
  165.8 10.1 %fusion.13 = f32[256,4096]{1,0:T(8,128)} fusion(bf16[256,2048]{1,0:T(8,128)(2,1)S(1)} %copy-done, bf16[4096,2048]{1,0:T(8,128)(2,1)} %all-gather.2.cloned.1.call-done), kind=kOutput, calls=%fused_computation.23 | convolution fusion | flops 4294967296 | bytes 22020096 | tf_op jit(solution)/shard_map/dot_general | solution.py:19
  175.9 2.4 select_convert_fusion
  178.3 0.1 collective-permute-start.1
  178.4 0.0 dynamic-slice-start
  178.4 0.0 all-to-all-done.1.fetched_ref
  178.4 5.5 %combine.1 = (bf16[256,2048]{1,0:T(8,128)(2,1)}, f32[256,1]{1,0:T(8,128)}) custom-call(s32[2,256]{1,0:T(2,128)} %get-tuple-element.6.slot_ref, s32[1,256]{1,0:T(1,128)} %bitcast.27, bf16[64,2,8,2048]{3,2,1,0:T(8,128)(2,1)} %all-to-all-done.1.fetched_ref, bf16[256,2048]{1,0:T(8,128)(2,1)} %bytes_ref.1), custom_call_target="tpu_custom_call" | custom-call | tf_op jit(solution)/shard_map/combine/pallas_call | solution.py:128
  183.9 1.0 reduce
  184.9 0.0 collective-permute-done.1
  184.9 0.0 dynamic-slice-done
  184.9 4.3 %multiply_reduce_fusion = (f32[256]{0:T(256)S(1)}, f32[256,2048]{1,0:T(8,128)}) fusion(bf16[256,2048]{1,0:T(8,128)(2,1)} %get-tuple-element.8.embedded_ref, f32[2048]{0:T(1024)S(1)} %dynamic-slice-done, bf16[256,2048]{1,0:T(8,128)(2,1)S(1)} %collective-permute-done.1, f32[256,4096]{1,0:T(8,128)} %fusion.13, pred[]{:T(512)S(6)} %eq.2), kind=kLoop, calls=%fused_computation.10 | loop fusion | flops 3669760 | bytes 8397825 | tf_op jit(solution)/shard_map/reduce_sum | solution.py:246
  189.3 0.5 collective-permute-start.2
  189.8 0.8 collective-permute-done.2
  190.6 0.8 copy.13.scale_ref
  191.4 0.8 copy.14.inner_ref
  192.2 5.6 %dispatch.1 = bf16[64,2,8,2048]{3,2,1,0:T(8,128)(2,1)} custom-call(s32[2,256]{1,0:T(2,128)} %get-tuple-element.6.slot_ref, f32[256,2048]{1,0:T(8,128)} %get-tuple-element.11.scaled_ref, bf16[256,2048]{1,0:T(8,128)(2,1)} %get-tuple-element.8.embedded_ref, f32[256,1]{1,0:T(8,128)} %copy.13.scale_ref, f32[256,1]{1,0:T(8,128)} %copy.14.inner_ref), custom_call_target="tpu_custom_call" | custom-call | tf_op jit(solution)/shard_map/dispatch/pallas_call | solution.py:168
  197.8 0.0 copy-start.1
  197.8 0.0 copy-start.2
  197.8 9.0 %all-to-all-start.2 = ((bf16[64,2,8,2048]{3,2,1,0:T(8,128)(2,1)}), bf16[64,2,8,2048]{3,2,1,0:T(8,128)(2,1)}, u32[]{:S(2)}, u32[]{:S(2)}) async-start(bf16[64,2,8,2048]{3,2,1,0:T(8,128)(2,1)} %dispatch.1), calls=%async_computation.2 | async-start | bytes 8388608 | tf_op jit(solution)/shard_map/all_to_all | solution.py:215
  206.9 0.0 copy-done.1
  206.9 0.3 collective-permute-start
  207.1 2.6 collective-permute-done
  209.8 0.0 copy-done.2
  209.8 11.3 %convolution_convert_fusion = bf16[256,2048]{1,0:T(8,128)(2,1)} fusion(bf16[4096,2048]{1,0:T(8,128)(2,1)} %all-gather.2.cloned.1.call-done, bf16[256,2048]{1,0:T(8,128)(2,1)S(1)} %collective-permute-done, bf16[256,2048]{1,0:T(8,128)(2,1)S(1)} %copy-done.1, f32[4096]{0:T(1024)S(1)} %copy-done.2, f32[256]{0:T(256)S(1)} %bitcast.26, pred[]{:T(512)S(6)} %eq.2), kind=kOutput, calls=%fused_computation.1 | convolution fusion | flops 4309123072 | bytes 19940352 | tf_op jit(solution)/shard_map/dot_general | solution.py:19
  221.1 43.7 %all-to-all-done.2.arrived_ref = bf16[64,2,8,2048]{3,2,1,0:T(8,128)(2,1)} async-done(((bf16[64,2,8,2048]{3,2,1,0:T(8,128)(2,1)}), bf16[64,2,8,2048]{3,2,1,0:T(8,128)(2,1)}, u32[]{:S(2)}, u32[]{:S(2)}) %all-to-all-start.2) | async-done | bytes 4194336 | tf_op jit(solution)/shard_map/all_to_all | solution.py:215
  264.8 11.0 %accumulate.1 = bf16[2,1024,2048]{2,1,0:T(8,128)(2,1)} custom-call(s32[64,128]{1,0:T(8,128)} %bitcast.18, bf16[64,2,8,2048]{3,2,1,0:T(8,128)(2,1)} %all-to-all-done.2.arrived_ref), custom_call_target="tpu_custom_call" | custom-call | tf_op jit(solution)/shard_map/accumulate/pallas_call | solution.py:200
  (3 shorter events, 0.0 us)
Async XLA Ops:
  7.2 158.6 %copy-start = (bf16[256,2048]{1,0:T(8,128)(2,1)S(1)}, bf16[256,2048]{1,0:T(8,128)(2,1)}, u32[]{:S(2)}) copy-start(bf16[256,2048]{1,0:T(8,128)(2,1)} %param.15) | copy-start | bytes 3145732
  7.2 158.6 %all-gather.2.cloned.1.call-start = ((), (), s32[]{:S(2)}) async-start(), calls=%async_computation.3 | async-start | bytes 17039360 | tf_op jit(solution)/shard_map/all_gather | solution.py:233
  42.0 136.4 %all-to-all-start.1 = ((bf16[64,2,8,2048]{3,2,1,0:T(8,128)(2,1)}), bf16[64,2,8,2048]{3,2,1,0:T(8,128)(2,1)}, u32[]{:S(2)}, u32[]{:S(2)}) async-start(bf16[64,2,8,2048]{3,2,1,0:T(8,128)(2,1)} %lookup.1), calls=%async_computation.1 | async-start | bytes 8388608 | tf_op jit(solution)/shard_map/all_to_all | solution.py:215
  178.3 6.6 %collective-permute-start.1 = (bf16[256,2048]{1,0:T(8,128)(2,1)S(1)}, bf16[256,2048]{1,0:T(8,128)(2,1)S(1)}, u32[]{:S(2)}, u32[]{:S(2)}) collective-permute-start(bf16[256,2048]{1,0:T(8,128)(2,1)S(1)} %select_convert_fusion), channel_id=1, source_target_pairs={{0,1},{1,0},{2,3},{3,2},{4,5},{5,4},{6,7},{7,6},{8,9},{9,8},{10,11... | collective-permute-start | bytes 3145736 | tf_op jit(solution)/shard_map/ppermute | solution.py:219
  178.4 6.5 %dynamic-slice-start = ((f32[4096]{0:T(1024)}, s32[]{:T(128)}), f32[2048]{0:T(1024)S(1)}, s32[]{:S(2)}) async-start(f32[4096]{0:T(1024)} %param.13, s32[]{:T(128)} %select_n.28), calls=%async_computation.4 | async-start | bytes 16896 | tf_op jit(solution)/shard_map/dynamic_slice | solution.py:244
  189.3 1.4 collective-permute-start.2
  197.8 9.1 %copy-start.1 = (bf16[256,2048]{1,0:T(8,128)(2,1)S(1)}, bf16[256,2048]{1,0:T(8,128)(2,1)}, u32[]{:S(2)}) copy-start(bf16[256,2048]{1,0:T(8,128)(2,1)} %get-tuple-element.8.embedded_ref) | copy-start | bytes 3145732
  197.8 12.0 %copy-start.2 = (f32[4096]{0:T(1024)S(1)}, f32[4096]{0:T(1024)}, u32[]{:S(2)}) copy-start(f32[4096]{0:T(1024)} %param.13) | copy-start | bytes 49156
  197.8 67.0 %all-to-all-start.2 = ((bf16[64,2,8,2048]{3,2,1,0:T(8,128)(2,1)}), bf16[64,2,8,2048]{3,2,1,0:T(8,128)(2,1)}, u32[]{:S(2)}, u32[]{:S(2)}) async-start(bf16[64,2,8,2048]{3,2,1,0:T(8,128)(2,1)} %dispatch.1), calls=%async_computation.2 | async-start | bytes 8388608 | tf_op jit(solution)/shard_map/all_to_all | solution.py:215
  206.9 2.9 %collective-permute-start = (bf16[256,2048]{1,0:T(8,128)(2,1)S(1)}, bf16[256,2048]{1,0:T(8,128)(2,1)S(1)}, u32[]{:S(2)}, u32[]{:S(2)}) collective-permute-start(bf16[256,2048]{1,0:T(8,128)(2,1)S(1)} %copy-done.1), channel_id=1, source_target_pairs={{0,1},{1,0},{2,3},{3,2},{4,5},{5,4},{6,7},{7,6},{8,9},{9,8},{10,11... | collective-permute-start | bytes 3145736 | tf_op jit(solution)/shard_map/ppermute | solution.py:219
Sparse Core Ops, SparseCore 0:
  10.9 154.8 all-gather.1
where the time goes:
time: 284 us; the launch traced here: 283 us
  waiting for transfers between devices  165 us (58%)
  Pallas kernels  34.7 us (12%)
  matrix products  21.4 us (8%)
  blocking collectives  20.1 us (7%)
  starting transfers between devices  16.7 us (6%)
  between operations  14.1 us (5%)
  other arithmetic  7.79 us (3%)
  local copies, waits for them, and re-layouts  2.88 us (1%)
    all_gather x1, waiting for transfers between devices, on_device(): weight = lax.all_gather(proj_weight, 'table', axis=0, tiled=True)  117 us
    all_to_all x2, waiting for transfers between devices, exchange(): return lax.all_to_all(array, axis, split_axis=0, concat_axis=0, tiled=True)  43.7 us
    dot_general x2, matrix products, dot(): lax.dot_general(a, b, (((ca,), (cb,)), ((), ())), preferred_element_type=...  21.4 us
    all_to_all x1, blocking collectives, exchange(): return lax.all_to_all(array, axis, split_axis=0, concat_axis=0, tiled=True)  20.1 us
    all_to_all x2, starting transfers between devices, exchange(): return lax.all_to_all(array, axis, split_axis=0, concat_axis=0, tiled=True)  15.8 us
    pallas_call x1, Pallas kernels, accumulate(): pl.pallas_call(functools.partial(accumulate_body, cap=cap), grid=(ngram,...  11 us
    pallas_call x1, Pallas kernels, lookup(): pl.pallas_call(functools.partial(lookup_body, cap=cap), grid=(ngram, widt...  10.8 us
  transfers between devices with their start and end apart: 6, of which 4 were waited for; matrix products, arithmetic and copies ran while one was open for 9% of the time, Pallas kernels for 6%

commit v1 on v0

v1 whole, which is shorter than its diff:
```python
import functools
import jax
import jax.numpy as jnp
from jax import lax
from jax.experimental import pallas as pl
from jax.experimental.pallas import tpu as pltpu
from jax.sharding import Mesh, PartitionSpec as P

eps = 1e-05
f32, bf16, i32 = jnp.float32, jnp.bfloat16, jnp.int32
LANES = 128
SPAN = 256
AXES = ("x", "y", "z")


def iota(shape, dim):
    return lax.broadcasted_iota(i32, shape, dim)


def dot(a, b, ca, cb):
    return lax.dot_general(a, b, (((ca,), (cb,)), ((), ())), preferred_element_type=f32)


def route_body(owner_ref, offset_ref, wanted_ref, slot_ref, *, groups, cap):
    ngram, _, tokens = owner_ref.shape
    earlier = (iota((tokens, tokens), 0) < iota((tokens, tokens), 1)).astype(f32).astype(bf16)
    lane = iota((groups, LANES), 1)
    wanted = jnp.full((groups, LANES), -1, i32)
    for k in range(ngram):
        owner = owner_ref[k]
        offset = offset_ref[k : k + 1, :]
        mine = jnp.broadcast_to(owner, (groups, tokens)) == iota((groups, tokens), 0)
        before = dot(mine.astype(f32).astype(bf16), earlier, 1, 0).astype(i32)
        rank = jnp.sum(jnp.where(mine, before, 0), axis=0, keepdims=True)
        slot_ref[k : k + 1, :] = owner * (ngram * cap) + k * cap + rank
        for r in range(cap):
            hit = jnp.where(mine & (before == r), offset + 1, 0)
            value = jnp.sum(hit, axis=1, keepdims=True) - 1
            wanted = jnp.where(lane == k * cap + r, value, wanted)
    wanted_ref[...] = wanted


def route(owner, offset, groups, cap):
    ngram, _, tokens = owner.shape
    return pl.pallas_call(
        functools.partial(route_body, groups=groups, cap=cap),
        out_shape=(
            jax.ShapeDtypeStruct((groups, LANES), i32),
            jax.ShapeDtypeStruct((ngram, tokens), i32),
        ),
        name="route",
    )(owner, offset)


def row_picks(asked, k, cap, rows):
    groups = asked.shape[0]
    total = groups * cap
    spread = (iota((total, groups), 0) // cap == iota((total, groups), 1)).astype(f32).astype(bf16)
    code = asked + 1
    high = (code >> 5).astype(f32).astype(bf16)
    low = (code & 31).astype(f32).astype(bf16)
    codes = dot(spread, high, 1, 0) * 32.0 + dot(spread, low, 1, 0)
    place = iota((total, LANES), 1) == k * cap + iota((total, LANES), 0) % cap
    column = jnp.sum(jnp.where(place, codes, 0.0), axis=1, keepdims=True).astype(i32) - 1
    return (column == iota((total, rows), 1)).astype(f32).astype(bf16)


def lookup_body(asked_ref, table_ref, out_ref, picks_ref, *, cap):
    k = pl.program_id(0)
    rows = table_ref.shape[1]

    @pl.when(pl.program_id(1) == 0)
    def _():
        picks_ref[...] = row_picks(asked_ref[...], k, cap, rows)

    out = dot(picks_ref[...], table_ref[0], 1, 0).astype(bf16)
    out_ref[...] = out.reshape(out_ref.shape)


def lookup(asked, tables, cap, block):
    groups = asked.shape[0]
    ngram, rows, width = tables.shape
    return pl.pallas_call(
        functools.partial(lookup_body, cap=cap),
        grid=(ngram, width // block),
        in_specs=[
            pl.BlockSpec((groups, LANES), lambda k, j: (0, 0)),
            pl.BlockSpec((1, rows, block), lambda k, j: (k, 0, j)),
        ],
        out_specs=pl.BlockSpec((groups, 1, cap, block), lambda k, j: (0, k, 0, j)),
        out_shape=jax.ShapeDtypeStruct((groups, ngram, cap, width), bf16),
        scratch_shapes=[pltpu.VMEM((groups * cap, rows), bf16)],
        name="lookup",
    )(asked, tables)


def slot_columns(slot_ref, slots):
    ngram, tokens = slot_ref.shape
    filled = jnp.concatenate([slot_ref[...], jnp.zeros((8 - ngram, tokens), i32)], axis=0)
    columns = filled.astype(f32).T.astype(i32)
    place = iota((tokens, slots), 1)
    hit = place == columns[:, 0:1]
    for k in range(1, ngram):
        hit = hit | (place == columns[:, k : k + 1])
    return hit.astype(f32).astype(bf16)


def side_by_side(ref):
    return jnp.concatenate([ref[i] for i in range(ref.shape[0])], axis=1)


def combine_body(
    slot_ref, ids_ref, fetched_ref, bytes_ref, dnormed_ref, gain_ref, out_ref, sums_ref, picks_ref, codes_ref
):
    tokens, slots = picks_ref.shape

    @pl.when(pl.program_id(0) == 0)
    def _():
        picks_ref[...] = slot_columns(slot_ref, slots)
        vocab = codes_ref.shape[0]
        codes_ref[...] = (iota((vocab, tokens), 0) == ids_ref[...]).astype(f32).astype(bf16)
        sums_ref[...] = jnp.zeros(sums_ref.shape, f32)

    block = fetched_ref.shape[-1]
    fetched = fetched_ref[...].reshape(slots, block)
    summed = dot(picks_ref[...], fetched, 1, 0) + dot(codes_ref[...], bytes_ref[...], 0, 0)
    embedded = summed.astype(bf16)
    for i in range(block // SPAN):
        out_ref[i] = embedded[:, i * SPAN : (i + 1) * SPAN]
    values = embedded.astype(f32)
    scaled = side_by_side(dnormed_ref).astype(f32) * gain_ref[...]
    square = jnp.sum(values * values, axis=1, keepdims=True)
    inner = jnp.sum(values * scaled, axis=1, keepdims=True)
    sums_ref[...] += jnp.where(iota(sums_ref.shape, 1) == 0, square, inner)


def combine(slot, ids, fetched, byte_table, dnormed, gain, block):
    groups, ngram, cap, width = fetched.shape
    tokens = slot.shape[1]
    vocab = byte_table.shape[0]
    slots = groups * ngram * cap
    return pl.pallas_call(
        combine_body,
        grid=(width // block,),
        in_specs=[
            pl.BlockSpec((ngram, tokens), lambda j: (0, 0)),
            pl.BlockSpec((1, tokens), lambda j: (0, 0)),
            pl.BlockSpec((groups, ngram, cap, block), lambda j: (0, 0, 0, j)),
            pl.BlockSpec((vocab, block), lambda j: (0, j)),
            pl.BlockSpec((block // SPAN, tokens, SPAN), lambda j: (j, 0, 0)),
            pl.BlockSpec((1, block), lambda j: (0, j)),
        ],
        out_specs=(
            pl.BlockSpec((block // SPAN, tokens, SPAN), lambda j: (j, 0, 0)),
            pl.BlockSpec((tokens, LANES), lambda j: (0, 0)),
        ),
        out_shape=(
            jax.ShapeDtypeStruct((width // SPAN, tokens, SPAN), bf16),
            jax.ShapeDtypeStruct((tokens, LANES), f32),
        ),
        scratch_shapes=[pltpu.VMEM((tokens, slots), bf16), pltpu.VMEM((vocab, tokens), bf16)],
        name="combine",
    )(slot, ids.reshape(1, tokens), fetched, byte_table, dnormed, gain)


def dispatch_body(
    slot_ref, dnormed_ref, gain_ref, embedded_ref, mine_ref, other_ref, out_ref, picks_ref, *, full_width
):
    slots, tokens = picks_ref.shape

    @pl.when(pl.program_id(0) == 0)
    def _():
        place = iota((slots, tokens), 0)
        hit = place == slot_ref[0:1, :]
        for k in range(1, slot_ref.shape[0]):
            hit = hit | (place == slot_ref[k : k + 1, :])
        picks_ref[...] = hit.astype(f32).astype(bf16)

    means = (mine_ref[...] + other_ref[...]) * (1.0 / full_width)
    scale = lax.rsqrt(means[:, 0:1] + eps)
    inner = means[:, 1:2]
    values = side_by_side(embedded_ref).astype(f32)
    scaled = side_by_side(dnormed_ref).astype(f32) * gain_ref[...]
    dembed = scale * scaled - values * (scale * scale * scale * inner)
    out = dot(picks_ref[...], dembed.astype(bf16), 1, 0).astype(bf16)
    out_ref[...] = out.reshape(out_ref.shape)


def dispatch(slot, dnormed, gain, embedded, mine, other, groups, cap, full_width, block):
    ngram, tokens = slot.shape
    width = embedded.shape[0] * SPAN
    slots = groups * ngram * cap
    return pl.pallas_call(
        functools.partial(dispatch_body, full_width=full_width),
        grid=(width // block,),
        in_specs=[
            pl.BlockSpec((ngram, tokens), lambda j: (0, 0)),
            pl.BlockSpec((block // SPAN, tokens, SPAN), lambda j: (j, 0, 0)),
            pl.BlockSpec((1, block), lambda j: (0, j)),
            pl.BlockSpec((block // SPAN, tokens, SPAN), lambda j: (j, 0, 0)),
            pl.BlockSpec((tokens, LANES), lambda j: (0, 0)),
            pl.BlockSpec((tokens, LANES), lambda j: (0, 0)),
        ],
        out_specs=pl.BlockSpec((groups, ngram, cap, block), lambda j: (0, 0, 0, j)),
        out_shape=jax.ShapeDtypeStruct((groups, ngram, cap, width), bf16),
        scratch_shapes=[pltpu.VMEM((slots, tokens), bf16)],
        name="dispatch",
    )(slot, dnormed, gain, embedded, mine, other)


def accumulate_body(asked_ref, arrived_ref, out_ref, picks_ref, *, cap):
    k = pl.program_id(0)
    rows = out_ref.shape[1]
    groups = asked_ref.shape[0]
    total = groups * cap

    @pl.when(pl.program_id(1) == 0)
    def _():
        spread = (iota((total, groups), 0) // cap == iota((total, groups), 1)).astype(f32).astype(bf16)
        code = asked_ref[...] + 1
        high = (code >> 5).astype(f32).astype(bf16)
        low = (code & 31).astype(f32).astype(bf16)
        codes = dot(high, spread, 0, 1) * 32.0 + dot(low, spread, 0, 1)
        place = iota((LANES, total), 0) == k * cap + iota((LANES, total), 1) % cap
        line = jnp.sum(jnp.where(place, codes, 0.0), axis=0, keepdims=True).astype(i32) - 1
        picks_ref[...] = (iota((rows, total), 0) == line).astype(f32).astype(bf16)

    arrived = arrived_ref[...].reshape(total, arrived_ref.shape[-1])
    out_ref[0] = dot(picks_ref[...], arrived, 1, 0).astype(bf16)


def accumulate(asked, arrived, rows, block):
    groups, ngram, cap, width = arrived.shape
    return pl.pallas_call(
        functools.partial(accumulate_body, cap=cap),
        grid=(ngram, width // block),
        in_specs=[
            pl.BlockSpec((groups, LANES), lambda k, j: (0, 0)),
            pl.BlockSpec((groups, 1, cap, block), lambda k, j: (0, k, 0, j)),
        ],
        out_specs=pl.BlockSpec((1, rows, block), lambda k, j: (k, 0, j)),
        out_shape=jax.ShapeDtypeStruct((ngram, rows, width), bf16),
        scratch_shapes=[pltpu.VMEM((rows, groups * cap), bf16)],
        name="accumulate",
    )(asked, arrived)


def exchange(array):
    return lax.all_to_all(array, AXES, split_axis=0, concat_axis=0, tiled=True)


def swapped(array):
    return lax.ppermute(array, "mp", [(0, 1), (1, 0)])


def shifted(array, turned, by):
    pairs = []
    for x in range(4):
        for y in range(4):
            for c in range(2):
                along_x = (c == 0) != turned
                to = ((x + by) % 4, y) if along_x else (x, (y + by) % 4)
                pairs.append(((x * 4 + y) * 2 + c, (to[0] * 4 + to[1]) * 2 + c))
    return lax.ppermute(array, ("x", "y", "mp"), pairs)


def shifted_z(array, by):
    return lax.ppermute(array, "z", [(i, (i + by) % 4) for i in range(4)])


def joined(blocks, here, dim):
    shape = list(blocks[0][0].shape)
    shape.insert(dim, 4)
    whole = jnp.zeros(shape, blocks[0][0].dtype)
    for block, away in blocks:
        whole = lax.dynamic_update_slice_in_dim(
            whole, jnp.expand_dims(block, dim), (here + away) % 4, dim
        )
    return whole


def product_body(*refs):
    cots, weight_ref, outs = refs[:4], refs[4], refs[5:]
    for cot_ref, out_ref in zip(cots, outs, strict=True):
        out_ref[...] = dot(cot_ref[...], weight_ref[...], 1, 1).astype(bf16)


def product(cots, weight, block):
    tokens, width = cots[0].shape
    rows = weight.shape[0]
    return pl.pallas_call(
        product_body,
        grid=(rows // block,),
        in_specs=[pl.BlockSpec((tokens, width), lambda j: (0, 0)) for _ in cots]
        + [pl.BlockSpec((block, width), lambda j: (j, 0))],
        out_specs=[pl.BlockSpec((tokens, block), lambda j: (0, j)) for _ in cots],
        out_shape=[jax.ShapeDtypeStruct((tokens, rows), bf16) for _ in cots],
        name="product",
    )(*cots, weight)


def feature_block(core, quarter, i):
    return jnp.where(core == 0, 4 * quarter + i, 4 * i + quarter)


def arrange_body(place_ref, *refs):
    core, ring = place_ref[0], place_ref[1]
    out_ref = refs[-1]
    for k, ref in enumerate(refs[:-1]):
        quarter = (ring + 4 - k) % 4
        for i in range(4):
            out_ref[feature_block(core, quarter, i)] = ref[:, i * SPAN : (i + 1) * SPAN]


def arrange(place, quarters):
    tokens = quarters[0].shape[0]
    return pl.pallas_call(
        arrange_body,
        in_specs=[pl.BlockSpec(memory_space=pltpu.SMEM)] + [pl.BlockSpec(memory_space=pltpu.VMEM)] * 4,
        out_shape=jax.ShapeDtypeStruct((16, tokens, SPAN), bf16),
        name="arrange",
    )(place, *quarters)


def normalize_body(place_ref, own_ref, theirs_ref, mine_ref, other_ref, gain_ref, *outs, full_width):
    core, ring = place_ref[0], place_ref[1]
    means = (mine_ref[...] + other_ref[...])[:, 0:1] * (1.0 / full_width)
    scale = lax.rsqrt(means + eps)
    for k, out_ref in enumerate(outs):
        quarter = (ring + k) % 4
        for i in range(4):
            at = feature_block(core, quarter, i)
            piece = jnp.where(at // 8 == core, own_ref[at % 8].astype(f32), theirs_ref[at % 8].astype(f32))
            out_ref[:, i * SPAN : (i + 1) * SPAN] = (piece * scale * gain_ref[at]).astype(bf16)


def normalize(place, own, theirs, mine, other, gain, full_width):
    tokens = own.shape[1]
    return pl.pallas_call(
        functools.partial(normalize_body, full_width=full_width),
        in_specs=[pl.BlockSpec(memory_space=pltpu.SMEM)] + [pl.BlockSpec(memory_space=pltpu.VMEM)] * 5,
        out_shape=[jax.ShapeDtypeStruct((tokens, 4 * SPAN), bf16)] * 4,
        name="normalize",
    )(place, own, theirs, mine, other, gain.reshape(16, 1, SPAN))


def on_device(
    hash_tables, byte_table, byte_ids, hash_owner, hash_offset, gain, proj_weight, cotangent
):
    groups = lax.axis_size(AXES)
    half = lax.axis_index("mp")
    first = half == 0
    x, y, z = (lax.axis_index(axis) for axis in AXES)
    ring, side = jnp.where(first, x, y), jnp.where(first, y, x)
    _, rows, width = hash_tables.shape
    tokens = byte_ids.shape[0]
    full_width = gain.shape[0]
    cap = 2 * tokens // groups
    block = 512

    gain_half = lax.dynamic_slice_in_dim(gain, half * width, width)[None, :]
    wanted, slot = route(jnp.swapaxes(hash_owner, 1, 2), hash_offset, groups, cap)
    asked = exchange(wanted.reshape(groups, 1, LANES)).reshape(groups, LANES)

    blocks = [(proj_weight, 0)] + [(shifted(proj_weight, True, -k), k) for k in (1, 3, 2)]
    weight = joined(blocks, side, 0)
    blocks = [(weight, 0)] + [(shifted_z(weight, -k), k) for k in (2, 1, 3)]
    weight = joined(blocks, z, 1).reshape(-1, width)
    cots = [cotangent] + [shifted(cotangent, False, -k) for k in (1, 2, 3)]

    looked = lookup(asked, hash_tables, cap, block)
    fetched = exchange(looked)

    products = product(cots, weight, 256)
    quarters = [products[0]] + [shifted(products[k], False, k) for k in (1, 2, 3)]
    place = jnp.stack([half, ring]).astype(i32)
    partial = arrange(place, quarters)
    two = partial.shape[0] // 2
    other = swapped(lax.dynamic_slice_in_dim(partial, (1 - half) * two, two))
    kept = lax.dynamic_slice_in_dim(partial, half * two, two)
    dnormed = (kept.astype(f32) + other.astype(f32)).astype(bf16)
    embedded, sums = combine(slot, byte_ids, fetched, byte_table, dnormed, gain_half, block)
    others = swapped(sums)
    theirs = swapped(embedded)
    sends = dispatch(
        slot, dnormed, gain_half, embedded, sums, others, groups, cap, full_width, block
    )

    pieces = normalize(place, embedded, theirs, sums, others, gain, full_width)
    turned = [pieces[0]] + [shifted(pieces[k], False, k) for k in (1, 2, 3)]
    arrived = exchange(sends)

    projected = dot(turned[0], weight, 1, 0)
    for k in (2, 1, 3):
        piece = dot(turned[k], weight, 1, 0).astype(bf16)
        projected = projected + shifted(piece, False, -k).astype(f32)
    table_grads = accumulate(asked, arrived, rows, block)
    return (projected.astype(bf16), table_grads)


def solution(mesh):
    sides = (4, 4, 4, 2)
    torus = Mesh(mesh.devices.reshape(sides), (*AXES, "mp"))

    return jax.shard_map(
        on_device,
        mesh=torus,
        in_specs=(
            P(None, AXES, "mp"),
            P(None, "mp"),
            P(AXES),
            P(None, AXES, None),
            P(None, AXES),
            P(),
            P(AXES, "mp"),
            P(AXES, "mp"),
        ),
        out_specs=(P(AXES, "mp"), P(None, AXES, "mp")),
        check_vma=False,
    )
```

time: 284 us -> 312 us (1.099)
  the two profiles are of different devices: /device:TPU:2 before, /device:TPU:50 now
where the time goes in v1:
time: 312 us; the launch traced here: 310 us
  waiting for transfers between devices  147 us (47%)
  starting transfers between devices  59.4 us (19%)
  Pallas kernels  50.7 us (16%)
  blocking collectives  21.2 us (7%)
  matrix products  15.2 us (5%)
  local copies, waits for them, and re-layouts  13.2 us (4%)
    ppermute x15, waiting for transfers between devices, shifted(): return lax.ppermute(array, ('x', 'y', 'mp'), pairs)  84.9 us
    ppermute x3, waiting for transfers between devices, shifted_z(): return lax.ppermute(array, 'z', [(i, (i + by) % 4) for i in range(4)])  57.3 us
    ppermute x15, starting transfers between devices, shifted(): return lax.ppermute(array, ('x', 'y', 'mp'), pairs)  29.6 us
    all_to_all x2, starting transfers between devices, exchange(): return lax.all_to_all(array, AXES, split_axis=0, concat_axis=0, tiled=True)  24 us
    all_to_all x1, blocking collectives, exchange(): return lax.all_to_all(array, AXES, split_axis=0, concat_axis=0, tiled=True)  21.2 us
    dot_general x4, matrix products, dot(): lax.dot_general(a, b, (((ca,), (cb,)), ((), ())), preferred_element_type=...  15.2 us
    pallas_call x1, Pallas kernels, accumulate(): pl.pallas_call(functools.partial(accumulate_body, cap=cap), grid=(ngram,...  11.4 us
    pallas_call x1, Pallas kernels, lookup(): pl.pallas_call(functools.partial(lookup_body, cap=cap), grid=(ngram, widt...  10.8 us
  transfers between devices with their start and end apart: 23, of which 13 were waited for; matrix products, arithmetic and copies ran while one was open for 9% of the time, Pallas kernels for 11%

profile of v1, /device:TPU:50, one launch (start us, length us, event | category | flops | bytes accessed | tf_op | source)
XLA Modules:
  0.0 310.4 jit_solution(15063334750075437031)
XLA Ops:
  0.6 0.5 collective-permute-start.3
  1.1 1.6 collective-permute-start.4
  2.7 1.3 collective-permute-start.5
  4.1 0.1 broadcast_in_dim.34
  4.2 1.0 bitcast_dynamic-update-slice_fusion.7
  5.1 2.1 collective-permute-done.3
  7.3 0.4 collective-permute-done.4
  7.8 3.7 %collective-permute-done.5 = bf16[64,2048]{1,0:T(8,128)(2,1)S(1)} collective-permute-done((bf16[64,2048]{1,0:T(8,128)(2,1)}, bf16[64,2048]{1,0:T(8,128)(2,1)S(1)}, u32[]{:S(2)}, u32[]{:S(2)}) %collective-permute-start.5) | collective-permute-done | bytes 262176 | tf_op jit(solution)/shard_map/ppermute | solution.py:264
  11.5 3.1 collective-permute-start.6
  14.5 1.8 route.1
  16.4 21.2 %all_to_all.15 = s32[64,1,128]{2,1,0:T(1,128)} all-to-all(s32[64,1,128]{2,1,0:T(1,128)} %bitcast.46), channel_id=1, replica_groups=mesh['x'=4,'y'=4,'z'=4,'mp'=2] {'x','y','z'}, dimensions={0} | all-to-all | bytes 65536 | tf_op jit(solution)/shard_map/all_to_all | solution.py:249
  37.6 10.8 %lookup.1 = bf16[64,2,8,2048]{3,2,1,0:T(8,128)(2,1)} custom-call(s32[64,128]{1,0:T(8,128)} %bitcast.41, bf16[2,1024,2048]{2,1,0:T(8,128)(2,1)} %table_ref.1), custom_call_target="tpu_custom_call" | custom-call | tf_op jit(solution)/shard_map/lookup/pallas_call | solution.py:83
  48.4 10.9 %all-to-all-start.1 = ((bf16[64,2,8,2048]{3,2,1,0:T(8,128)(2,1)}), bf16[64,2,8,2048]{3,2,1,0:T(8,128)(2,1)}, u32[]{:S(2)}, u32[]{:S(2)}) async-start(bf16[64,2,8,2048]{3,2,1,0:T(8,128)(2,1)} %lookup.1), calls=%async_computation.1 | async-start | bytes 8388608 | tf_op jit(solution)/shard_map/all_to_all | solution.py:249
  59.4 0.6 collective-permute-start.7
  60.0 0.5 collective-permute-start
  60.5 2.5 collective-permute-start.1
  63.0 1.5 collective-permute-start.8
  64.5 2.5 broadcast_in_dim.33
  67.0 1.1 bitcast_dynamic-update-slice_fusion.2
  68.1 1.9 collective-permute-start.2
  70.0 1.1 bitcast_dynamic-update-slice_fusion.1
  71.0 57.3 %collective-permute-done.7 = bf16[4,64,2048]{2,1,0:T(8,128)(2,1)S(1)} collective-permute-done((bf16[4,64,2048]{2,1,0:T(8,128)(2,1)S(1)}, bf16[4,64,2048]{2,1,0:T(8,128)(2,1)S(1)}, u32[]{:S(2)}, u32[]{:S(2)}) %collective-permute-start.7) | collective-permute-done | bytes 1048608 | tf_op jit(solution)/shard_map/ppermute | solution.py:268
  128.4 1.1 bitcast_dynamic-update-slice_fusion
  129.4 1.0 bitcast_dynamic-update-slice_fusion.3
  130.5 2.0 collective-permute-done.1.refs_2_
  132.5 1.0 copy-done.2
  133.4 8.5 %product.1 = (bf16[256,1024]{1,0:T(8,128)(2,1)}, bf16[256,1024]{1,0:T(8,128)(2,1)}, bf16[256,1024]{1,0:T(8,128)(2,1)}, bf16[256,1024]{1,0:T(8,128)(2,1)}) custom-call(bf16[256,2048]{1,0:T(8,128)(2,1)} %refs_0_.1, bf16[256,2048]{1,0:T(8,128)(2,1)} %collective-permute-done.refs_1_, bf16[256,2048]{1,0:T(8,128)(2,1)} %collective-permute-done.1.refs_2_, ...), custom_call_target="tpu_custom_call" | custom-call | tf_op jit(solution)/shard_map/product/pallas_call | solution.py:291
  142.0 0.0 collective-permute-start.9
  142.0 1.4 collective-permute-start.10
  143.4 2.5 collective-permute-start.11
  145.9 0.6 pad_add_fusion.place_ref
  146.5 4.9 %collective-permute-done.9.refs_1_ = bf16[256,1024]{1,0:T(8,128)(2,1)S(1)} collective-permute-done((bf16[256,1024]{1,0:T(8,128)(2,1)}, bf16[256,1024]{1,0:T(8,128)(2,1)S(1)}, u32[]{:S(2)}, u32[]{:S(2)}) %collective-permute-start.9) | collective-permute-done | bytes 524320 | tf_op jit(solution)/shard_map/ppermute | solution.py:264
  151.4 1.7 collective-permute-done.10.refs_2_
  153.1 5.4 %collective-permute-done.11.refs_3_ = bf16[256,1024]{1,0:T(8,128)(2,1)S(1)} collective-permute-done((bf16[256,1024]{1,0:T(8,128)(2,1)}, bf16[256,1024]{1,0:T(8,128)(2,1)S(1)}, u32[]{:S(2)}, u32[]{:S(2)}) %collective-permute-start.11) | collective-permute-done | bytes 524320 | tf_op jit(solution)/shard_map/ppermute | solution.py:264
  158.5 0.8 copy-done.5
  159.3 3.0 arrange.1
  162.3 1.3 constant_dynamic-slice_fusion
  163.6 0.1 collective-permute-start.12
  163.7 0.6 dynamic_slice.11
  164.3 2.0 collective-permute-done.12
  166.4 2.4 add_convert_fusion.dnormed_ref
  168.8 5.9 %combine.1 = (bf16[8,256,256]{2,1,0:T(8,128)(2,1)}, f32[256,128]{1,0:T(8,128)}) custom-call(s32[2,256]{1,0:T(2,128)} %get-tuple-element.14.slot_ref, s32[1,256]{1,0:T(1,128)} %bitcast.48, bf16[64,2,8,2048]{3,2,1,0:T(8,128)(2,1)} %all-to-all-done.1.fetched_ref, bf16[256,2048]{1,0:T(8,128)(2,1)} %bytes_ref.1, ...), custom_call_target="tpu_custom_call" | custom-call | tf_op jit(solution)/shard_map/combine/pallas_call | solution.py:142
  174.7 0.1 collective-permute-start.13
  174.8 0.4 collective-permute-start.14
  175.2 2.5 collective-permute-done.14.other_ref
  177.8 0.7 copy-done.6
  178.4 5.5 %dispatch.1 = bf16[64,2,8,2048]{3,2,1,0:T(8,128)(2,1)} custom-call(s32[2,256]{1,0:T(2,128)} %get-tuple-element.14.slot_ref, bf16[8,256,256]{2,1,0:T(8,128)(2,1)} %add_convert_fusion.dnormed_ref, f32[1,2048]{1,0:T(1,128)} %bitcast.44, bf16[8,256,256]{2,1,0:T(8,128)(2,1)} %get-tuple-element.20.own_ref.embedded_ref, f32[256,128]{1,0:T(8,128)} %get-tuple-element.21.mine_ref, ...), custom_call_target="tpu_custom_call" | custom-call | tf_op jit(solution)/shard_map/dispatch/pallas_call | solution.py:193
  183.9 13.1 %all-to-all-start.2 = ((bf16[64,2,8,2048]{3,2,1,0:T(8,128)(2,1)}), bf16[64,2,8,2048]{3,2,1,0:T(8,128)(2,1)}, u32[]{:S(2)}, u32[]{:S(2)}) async-start(bf16[64,2,8,2048]{3,2,1,0:T(8,128)(2,1)} %dispatch.1), calls=%async_computation.2 | async-start | bytes 8388608 | tf_op jit(solution)/shard_map/all_to_all | solution.py:249
  197.1 1.0 copy-done
  198.0 3.7 %normalize.1 = (bf16[256,1024]{1,0:T(8,128)(2,1)}, bf16[256,1024]{1,0:T(8,128)(2,1)}, bf16[256,1024]{1,0:T(8,128)(2,1)}, bf16[256,1024]{1,0:T(8,128)(2,1)}) custom-call(s32[2]{0:T(128)} %pad_add_fusion.place_ref, bf16[8,256,256]{2,1,0:T(8,128)(2,1)} %get-tuple-element.20.own_ref.embedded_ref, bf16[8,256,256]{2,1,0:T(8,128)(2,1)} %copy-done, ...), custom_call_target="tpu_custom_call" | custom-call | tf_op jit(solution)/shard_map/normalize/pallas_call | solution.py:339
  201.7 0.5 collective-permute-start.19
  202.2 1.5 collective-permute-start.17
  203.8 3.5 %collective-permute-start.15 = (bf16[256,1024]{1,0:T(8,128)(2,1)}, bf16[256,1024]{1,0:T(8,128)(2,1)S(1)}, u32[]{:S(2)}, u32[]{:S(2)}) collective-permute-start(bf16[256,1024]{1,0:T(8,128)(2,1)} %get-tuple-element.23), channel_id=1, source_target_pairs={{0,64},{1,17},{8,72},{9,25},{16,80},{17,1},{24,88},{25,9},{32,96},... | collective-permute-start | bytes 1572872 | tf_op jit(solution)/shard_map/ppermute | solution.py:264
  207.3 43.7 %collective-permute-done.19 = bf16[256,1024]{1,0:T(8,128)(2,1)S(1)} collective-permute-done((bf16[256,1024]{1,0:T(8,128)(2,1)}, bf16[256,1024]{1,0:T(8,128)(2,1)S(1)}, u32[]{:S(2)}, u32[]{:S(2)}) %collective-permute-start.19) | collective-permute-done | bytes 524320 | tf_op jit(solution)/shard_map/ppermute | solution.py:264
  250.9 3.4 %convolution_convert_fusion = bf16[256,2048]{1,0:T(8,128)(2,1)S(1)} fusion(bf16[256,1024]{1,0:T(8,128)(2,1)S(1)} %collective-permute-done.19, bf16[1024,2048]{1,0:T(8,128)(2,1)} %bitcast.18.refs_4_), kind=kOutput, calls=%fused_computation.4 | convolution fusion | flops 1074266112 | bytes 5767168 | tf_op jit(solution)/shard_map/dot_general | solution.py:21
  254.4 10.3 %collective-permute-start.20 = (bf16[256,2048]{1,0:T(8,128)(2,1)S(1)}, bf16[256,2048]{1,0:T(8,128)(2,1)S(1)}, u32[]{:S(2)}, u32[]{:S(2)}) collective-permute-start(bf16[256,2048]{1,0:T(8,128)(2,1)S(1)} %convolution_convert_fusion), channel_id=1, source_target_pairs={{0,32},{1,9},{8,40},{9,17},{16,48},{17,25},{24,56},{25,1},{32,64},... | collective-permute-start | bytes 3145736 | tf_op jit(solution)/shard_map/ppermute | solution.py:264
  264.6 3.4 %convolution_convert_fusion.1 = bf16[256,2048]{1,0:T(8,128)(2,1)S(1)} fusion(bf16[256,1024]{1,0:T(8,128)(2,1)S(1)} %collective-permute-done.17, bf16[1024,2048]{1,0:T(8,128)(2,1)} %bitcast.18.refs_4_), kind=kOutput, calls=%fused_computation.5 | convolution fusion | flops 1074266112 | bytes 5767168 | tf_op jit(solution)/shard_map/dot_general | solution.py:21
  268.1 0.1 collective-permute-start.18
  268.2 3.5 %convolution_convert_fusion.2 = bf16[256,2048]{1,0:T(8,128)(2,1)S(1)} fusion(bf16[256,1024]{1,0:T(8,128)(2,1)S(1)} %collective-permute-done.15, bf16[1024,2048]{1,0:T(8,128)(2,1)} %bitcast.18.refs_4_), kind=kOutput, calls=%fused_computation.6 | convolution fusion | flops 1074266112 | bytes 5767168 | tf_op jit(solution)/shard_map/dot_general | solution.py:21
  271.7 1.5 collective-permute-start.16
  273.2 15.0 %collective-permute-done.20 = bf16[256,2048]{1,0:T(8,128)(2,1)S(1)} collective-permute-done((bf16[256,2048]{1,0:T(8,128)(2,1)S(1)}, bf16[256,2048]{1,0:T(8,128)(2,1)S(1)}, u32[]{:S(2)}, u32[]{:S(2)}) %collective-permute-start.20) | collective-permute-done | bytes 1048608 | tf_op jit(solution)/shard_map/ppermute | solution.py:264
  288.2 6.0 %collective-permute-done.18 = bf16[256,2048]{1,0:T(8,128)(2,1)S(1)} collective-permute-done((bf16[256,2048]{1,0:T(8,128)(2,1)S(1)}, bf16[256,2048]{1,0:T(8,128)(2,1)S(1)}, u32[]{:S(2)}, u32[]{:S(2)}) %collective-permute-start.18) | collective-permute-done | bytes 1048608 | tf_op jit(solution)/shard_map/ppermute | solution.py:264
  294.2 4.8 %fusion.2 = bf16[256,2048]{1,0:T(8,128)(2,1)} fusion(bf16[256,1024]{1,0:T(8,128)(2,1)S(1)} %copy-done.8, bf16[1024,2048]{1,0:T(8,128)(2,1)} %bitcast.18.refs_4_, bf16[256,2048]{1,0:T(8,128)(2,1)S(1)} %collective-permute-done.20, bf16[256,2048]{1,0:T(8,128)(2,1)S(1)} %collective-permute-done.18, bf16[256,2048]{1,0:T(8,128)(2,1)S(1)} %collective-permute-done.16), kind=kOutput, calls=%fused_computation.3 | convolution fusion | flops 1077411840 | bytes 8912896 | tf_op jit(solution)/shard_map/dot_general | solution.py:21
  299.0 11.4 %accumulate.1 = bf16[2,1024,2048]{2,1,0:T(8,128)(2,1)} custom-call(s32[64,128]{1,0:T(8,128)} %bitcast.42, bf16[64,2,8,2048]{3,2,1,0:T(8,128)(2,1)} %all-to-all-done.2.arrived_ref), custom_call_target="tpu_custom_call" | custom-call | tf_op jit(solution)/shard_map/accumulate/pallas_call | solution.py:234
  (27 shorter events, 0.1 us)
Async XLA Ops:
  0.6 6.7 %collective-permute-start.3 = (bf16[64,2048]{1,0:T(8,128)(2,1)}, bf16[64,2048]{1,0:T(8,128)(2,1)S(1)}, u32[]{:S(2)}, u32[]{:S(2)}) collective-permute-start(bf16[64,2048]{1,0:T(8,128)(2,1)} %param.14), channel_id=1, source_target_pairs={{0,24},{1,97},{8,0},{9,105},{16,8},{17,113},{24,16},{25,121},{32,5... | collective-permute-start | bytes 786440 | tf_op jit(solution)/shard_map/ppermute | solution.py:264
  1.1 6.6 %collective-permute-start.4 = (bf16[64,2048]{1,0:T(8,128)(2,1)}, bf16[64,2048]{1,0:T(8,128)(2,1)S(1)}, u32[]{:S(2)}, u32[]{:S(2)}) collective-permute-start(bf16[64,2048]{1,0:T(8,128)(2,1)} %param.14), channel_id=1, source_target_pairs={{0,8},{1,33},{8,16},{9,41},{16,24},{17,49},{24,0},{25,57},{32,40},... | collective-permute-start | bytes 786440 | tf_op jit(solution)/shard_map/ppermute | solution.py:264
  2.7 8.7 %collective-permute-start.5 = (bf16[64,2048]{1,0:T(8,128)(2,1)}, bf16[64,2048]{1,0:T(8,128)(2,1)S(1)}, u32[]{:S(2)}, u32[]{:S(2)}) collective-permute-start(bf16[64,2048]{1,0:T(8,128)(2,1)} %param.14), channel_id=1, source_target_pairs={{0,16},{1,65},{8,24},{9,73},{16,0},{17,81},{24,8},{25,89},{32,48},... | collective-permute-start | bytes 786440 | tf_op jit(solution)/shard_map/ppermute | solution.py:264
  11.5 56.6 %collective-permute-start.6 = (bf16[4,64,2048]{2,1,0:T(8,128)(2,1)S(1)}, bf16[4,64,2048]{2,1,0:T(8,128)(2,1)S(1)}, u32[]{:S(2)}, u32[]{:S(2)}) collective-permute-start(bf16[4,64,2048]{2,1,0:T(8,128)(2,1)S(1)} %bitcast_dynamic-update-slice_fusion.4), channel_id=1, source_target_pairs={{0,4},{2,6},{4,0},{6,2},{1,5},{3,7},{5,1},{7,3},{8,12},{10,14},{12... | collective-permute-start | bytes 3145736 | tf_op jit(solution)/shard_map/ppermute | solution.py:268
  48.4 120.4 %all-to-all-start.1 = ((bf16[64,2,8,2048]{3,2,1,0:T(8,128)(2,1)}), bf16[64,2,8,2048]{3,2,1,0:T(8,128)(2,1)}, u32[]{:S(2)}, u32[]{:S(2)}) async-start(bf16[64,2,8,2048]{3,2,1,0:T(8,128)(2,1)} %lookup.1), calls=%async_computation.1 | async-start | bytes 8388608 | tf_op jit(solution)/shard_map/all_to_all | solution.py:249
  59.4 69.0 %collective-permute-start.7 = (bf16[4,64,2048]{2,1,0:T(8,128)(2,1)S(1)}, bf16[4,64,2048]{2,1,0:T(8,128)(2,1)S(1)}, u32[]{:S(2)}, u32[]{:S(2)}) collective-permute-start(bf16[4,64,2048]{2,1,0:T(8,128)(2,1)S(1)} %bitcast_dynamic-update-slice_fusion.4), channel_id=1, source_target_pairs={{0,6},{2,0},{4,2},{6,4},{1,7},{3,1},{5,3},{7,5},{8,14},{10,8},{12,... | collective-permute-start | bytes 3145736 | tf_op jit(solution)/shard_map/ppermute | solution.py:268
  60.0 70.5 %collective-permute-start = (bf16[256,2048]{1,0:T(8,128)(2,1)}, bf16[256,2048]{1,0:T(8,128)(2,1)}, u32[]{:S(2)}, u32[]{:S(2)}) collective-permute-start(bf16[256,2048]{1,0:T(8,128)(2,1)} %refs_0_.1), channel_id=1, source_target_pairs={{0,96},{1,25},{8,104},{9,1},{16,112},{17,9},{24,120},{25,17},{32,0... | collective-permute-start | bytes 3145736 | tf_op jit(solution)/shard_map/ppermute | solution.py:264
  60.5 72.0 %collective-permute-start.1 = (bf16[256,2048]{1,0:T(8,128)(2,1)}, bf16[256,2048]{1,0:T(8,128)(2,1)}, u32[]{:S(2)}, u32[]{:S(2)}) collective-permute-start(bf16[256,2048]{1,0:T(8,128)(2,1)} %refs_0_.1), channel_id=1, source_target_pairs={{0,64},{1,17},{8,72},{9,25},{16,80},{17,1},{24,88},{25,9},{32,96},... | collective-permute-start | bytes 3145736 | tf_op jit(solution)/shard_map/ppermute | solution.py:264
  63.0 5.1 %copy-start.1 = (bf16[256,2048]{1,0:T(8,128)(2,1)S(1)}, bf16[256,2048]{1,0:T(8,128)(2,1)}, u32[]{:S(2)}) copy-start(bf16[256,2048]{1,0:T(8,128)(2,1)} %refs_0_.1) | copy-start | bytes 3145732
  63.0 66.4 %collective-permute-start.8 = (bf16[4,64,2048]{2,1,0:T(8,128)(2,1)S(1)}, bf16[4,64,2048]{2,1,0:T(8,128)(2,1)S(1)}, u32[]{:S(2)}, u32[]{:S(2)}) collective-permute-start(bf16[4,64,2048]{2,1,0:T(8,128)(2,1)S(1)} %bitcast_dynamic-update-slice_fusion.4), channel_id=1, source_target_pairs={{0,2},{2,4},{4,6},{6,0},{1,3},{3,5},{5,7},{7,1},{8,10},{10,12},{12... | collective-permute-start | bytes 3145736 | tf_op jit(solution)/shard_map/ppermute | solution.py:268
  68.1 64.4 %collective-permute-start.2 = (bf16[256,2048]{1,0:T(8,128)(2,1)S(1)}, bf16[256,2048]{1,0:T(8,128)(2,1)S(1)}, u32[]{:S(2)}, u32[]{:S(2)}) collective-permute-start(bf16[256,2048]{1,0:T(8,128)(2,1)S(1)} %copy-done.1), channel_id=1, source_target_pairs={{0,32},{1,9},{8,40},{9,17},{16,48},{17,25},{24,56},{25,1},{32,64},... | collective-permute-start | bytes 3145736 | tf_op jit(solution)/shard_map/ppermute | solution.py:264
  132.5 1.0 copy-start.2
  142.0 21.7 %copy-start.7 = (f32[4096]{0:T(1024)S(1)}, f32[4096]{0:T(1024)}, u32[]{:S(2)}) copy-start(f32[4096]{0:T(1024)} %param.13) | copy-start | bytes 49156
  142.0 9.4 %collective-permute-start.9 = (bf16[256,1024]{1,0:T(8,128)(2,1)}, bf16[256,1024]{1,0:T(8,128)(2,1)S(1)}, u32[]{:S(2)}, u32[]{:S(2)}) collective-permute-start(bf16[256,1024]{1,0:T(8,128)(2,1)} %get-tuple-element.17), channel_id=1, source_target_pairs={{0,32},{1,9},{8,40},{9,17},{16,48},{17,25},{24,56},{25,1},{32,64},... | collective-permute-start | bytes 1572872 | tf_op jit(solution)/shard_map/ppermute | solution.py:264
  142.0 11.1 %collective-permute-start.10 = (bf16[256,1024]{1,0:T(8,128)(2,1)}, bf16[256,1024]{1,0:T(8,128)(2,1)S(1)}, u32[]{:S(2)}, u32[]{:S(2)}) collective-permute-start(bf16[256,1024]{1,0:T(8,128)(2,1)} %get-tuple-element.18), channel_id=1, source_target_pairs={{0,64},{1,17},{8,72},{9,25},{16,80},{17,1},{24,88},{25,9},{32,96},... | collective-permute-start | bytes 1572872 | tf_op jit(solution)/shard_map/ppermute | solution.py:264
  143.4 15.1 %collective-permute-start.11 = (bf16[256,1024]{1,0:T(8,128)(2,1)}, bf16[256,1024]{1,0:T(8,128)(2,1)S(1)}, u32[]{:S(2)}, u32[]{:S(2)}) collective-permute-start(bf16[256,1024]{1,0:T(8,128)(2,1)} %get-tuple-element.19), channel_id=1, source_target_pairs={{0,96},{1,25},{8,104},{9,1},{16,112},{17,9},{24,120},{25,17},{32,0... | collective-permute-start | bytes 1572872 | tf_op jit(solution)/shard_map/ppermute | solution.py:264
  151.4 7.1 %copy-start.3 = (bf16[256,1024]{1,0:T(8,128)(2,1)}, bf16[256,1024]{1,0:T(8,128)(2,1)S(1)}, u32[]{:S(2)}) copy-start(bf16[256,1024]{1,0:T(8,128)(2,1)S(1)} %collective-permute-done.9.refs_1_) | copy-start | bytes 1572868
  153.1 5.4 %copy-start.4 = (bf16[256,1024]{1,0:T(8,128)(2,1)}, bf16[256,1024]{1,0:T(8,128)(2,1)S(1)}, u32[]{:S(2)}) copy-start(bf16[256,1024]{1,0:T(8,128)(2,1)S(1)} %collective-permute-done.10.refs_2_) | copy-start | bytes 1572868
  158.5 0.8 copy-start.5
  163.6 2.7 collective-permute-start.12
  174.7 22.3 %collective-permute-start.13 = (bf16[8,256,256]{2,1,0:T(8,128)(2,1)}, bf16[8,256,256]{2,1,0:T(8,128)(2,1)S(1)}, u32[]{:S(2)}, u32[]{:S(2)}) collective-permute-start(bf16[8,256,256]{2,1,0:T(8,128)(2,1)} %get-tuple-element.20.own_ref.embedded_ref), channel_id=1, source_target_pairs={{0,1},{1,0},{2,3},{3,2},{4,5},{5,4},{6,7},{7,6},{8,9},{9,8},{10,11... | collective-permute-start | bytes 3145736 | tf_op jit(solution)/shard_map/ppermute | solution.py:253
  174.8 2.9 collective-permute-start.14
  177.8 0.7 copy-start.6
  183.9 115.1 %all-to-all-start.2 = ((bf16[64,2,8,2048]{3,2,1,0:T(8,128)(2,1)}), bf16[64,2,8,2048]{3,2,1,0:T(8,128)(2,1)}, u32[]{:S(2)}, u32[]{:S(2)}) async-start(bf16[64,2,8,2048]{3,2,1,0:T(8,128)(2,1)} %dispatch.1), calls=%async_computation.2 | async-start | bytes 8388608 | tf_op jit(solution)/shard_map/all_to_all | solution.py:249
  197.1 1.0 copy-start
  201.7 49.2 %collective-permute-start.19 = (bf16[256,1024]{1,0:T(8,128)(2,1)}, bf16[256,1024]{1,0:T(8,128)(2,1)S(1)}, u32[]{:S(2)}, u32[]{:S(2)}) collective-permute-start(bf16[256,1024]{1,0:T(8,128)(2,1)} %get-tuple-element.25), channel_id=1, source_target_pairs={{0,96},{1,25},{8,104},{9,1},{16,112},{17,9},{24,120},{25,17},{32,0... | collective-permute-start | bytes 1572872 | tf_op jit(solution)/shard_map/ppermute | solution.py:264
  202.2 62.4 %collective-permute-start.17 = (bf16[256,1024]{1,0:T(8,128)(2,1)}, bf16[256,1024]{1,0:T(8,128)(2,1)S(1)}, u32[]{:S(2)}, u32[]{:S(2)}) collective-permute-start(bf16[256,1024]{1,0:T(8,128)(2,1)} %get-tuple-element.24), channel_id=1, source_target_pairs={{0,32},{1,9},{8,40},{9,17},{16,48},{17,25},{24,56},{25,1},{32,64},... | collective-permute-start | bytes 1572872 | tf_op jit(solution)/shard_map/ppermute | solution.py:264
  203.8 64.4 %collective-permute-start.15 = (bf16[256,1024]{1,0:T(8,128)(2,1)}, bf16[256,1024]{1,0:T(8,128)(2,1)S(1)}, u32[]{:S(2)}, u32[]{:S(2)}) collective-permute-start(bf16[256,1024]{1,0:T(8,128)(2,1)} %get-tuple-element.23), channel_id=1, source_target_pairs={{0,64},{1,17},{8,72},{9,25},{16,80},{17,1},{24,88},{25,9},{32,96},... | collective-permute-start | bytes 1572872 | tf_op jit(solution)/shard_map/ppermute | solution.py:264
  254.4 33.9 %collective-permute-start.20 = (bf16[256,2048]{1,0:T(8,128)(2,1)S(1)}, bf16[256,2048]{1,0:T(8,128)(2,1)S(1)}, u32[]{:S(2)}, u32[]{:S(2)}) collective-permute-start(bf16[256,2048]{1,0:T(8,128)(2,1)S(1)} %convolution_convert_fusion), channel_id=1, source_target_pairs={{0,32},{1,9},{8,40},{9,17},{16,48},{17,25},{24,56},{25,1},{32,64},... | collective-permute-start | bytes 3145736 | tf_op jit(solution)/shard_map/ppermute | solution.py:264
  268.1 26.1 %copy-start.8 = (bf16[256,1024]{1,0:T(8,128)(2,1)S(1)}, bf16[256,1024]{1,0:T(8,128)(2,1)}, u32[]{:S(2)}) copy-start(bf16[256,1024]{1,0:T(8,128)(2,1)} %get-tuple-element.22) | copy-start | bytes 1572868
  268.1 26.1 %collective-permute-start.18 = (bf16[256,2048]{1,0:T(8,128)(2,1)S(1)}, bf16[256,2048]{1,0:T(8,128)(2,1)S(1)}, u32[]{:S(2)}, u32[]{:S(2)}) collective-permute-start(bf16[256,2048]{1,0:T(8,128)(2,1)S(1)} %convolution_convert_fusion.1), channel_id=1, source_target_pairs={{0,96},{1,25},{8,104},{9,1},{16,112},{17,9},{24,120},{25,17},{32,0... | collective-permute-start | bytes 3145736 | tf_op jit(solution)/shard_map/ppermute | solution.py:264
  271.7 22.5 %collective-permute-start.16 = (bf16[256,2048]{1,0:T(8,128)(2,1)S(1)}, bf16[256,2048]{1,0:T(8,128)(2,1)S(1)}, u32[]{:S(2)}, u32[]{:S(2)}) collective-permute-start(bf16[256,2048]{1,0:T(8,128)(2,1)S(1)} %convolution_convert_fusion.2), channel_id=1, source_target_pairs={{0,64},{1,17},{8,72},{9,25},{16,80},{17,1},{24,88},{25,9},{32,96},... | collective-permute-start | bytes 3145736 | tf_op jit(solution)/shard_map/ppermute | solution.py:264

commit v2 on v1

--- a/solution.py
+++ b/solution.py
@@ -110,7 +110,7 @@
 
 
 def combine_body(
-    slot_ref, ids_ref, fetched_ref, bytes_ref, dnormed_ref, gain_ref, out_ref, sums_ref, picks_ref, codes_ref
+    slot_ref, ids_ref, fetched_ref, bytes_ref, out_ref, square_ref, picks_ref, codes_ref
 ):
     tokens, slots = picks_ref.shape
 
@@ -119,7 +119,7 @@
         picks_ref[...] = slot_columns(slot_ref, slots)
         vocab = codes_ref.shape[0]
         codes_ref[...] = (iota((vocab, tokens), 0) == ids_ref[...]).astype(f32).astype(bf16)
-        sums_ref[...] = jnp.zeros(sums_ref.shape, f32)
+        square_ref[...] = jnp.zeros(square_ref.shape, f32)
 
     block = fetched_ref.shape[-1]
     fetched = fetched_ref[...].reshape(slots, block)
@@ -128,13 +128,10 @@
     for i in range(block // SPAN):
         out_ref[i] = embedded[:, i * SPAN : (i + 1) * SPAN]
     values = embedded.astype(f32)
-    scaled = side_by_side(dnormed_ref).astype(f32) * gain_ref[...]
-    square = jnp.sum(values * values, axis=1, keepdims=True)
-    inner = jnp.sum(values * scaled, axis=1, keepdims=True)
-    sums_ref[...] += jnp.where(iota(sums_ref.shape, 1) == 0, square, inner)
-
-
-def combine(slot, ids, fetched, byte_table, dnormed, gain, block):
+    square_ref[...] += jnp.sum(values * values, axis=1, keepdims=True)
+
+
+def combine(slot, ids, fetched, byte_table, block):
     groups, ngram, cap, width = fetched.shape
     tokens = slot.shape[1]
     vocab = byte_table.shape[0]
@@ -147,8 +144,6 @@
             pl.BlockSpec((1, tokens), lambda j: (0, 0)),
             pl.BlockSpec((groups, ngram, cap, block), lambda j: (0, 0, 0, j)),
             pl.BlockSpec((vocab, block), lambda j: (0, j)),
-            pl.BlockSpec((block // SPAN, tokens, SPAN), lambda j: (j, 0, 0)),
-            pl.BlockSpec((1, block), lambda j: (0, j)),
         ],
         out_specs=(
             pl.BlockSpec((block // SPAN, tokens, SPAN), lambda j: (j, 0, 0)),
@@ -160,11 +155,11 @@
         ),
         scratch_shapes=[pltpu.VMEM((tokens, slots), bf16), pltpu.VMEM((vocab, tokens), bf16)],
         name="combine",
-    )(slot, ids.reshape(1, tokens), fetched, byte_table, dnormed, gain)
+    )(slot, ids.reshape(1, tokens), fetched, byte_table)
 
 
 def dispatch_body(
-    slot_ref, dnormed_ref, gain_ref, embedded_ref, mine_ref, other_ref, out_ref, picks_ref, *, full_width
+    slot_ref, kept_ref, other_ref, gain_ref, embedded_ref, sq0_ref, sq1_ref, in0_ref, in1_ref, out_ref, picks_ref, *, full_width
 ):
     slots, tokens = picks_ref.shape
 
@@ -176,36 +171,41 @@
             hit = hit | (place == slot_ref[k : k + 1, :])
         picks_ref[...] = hit.astype(f32).astype(bf16)
 
-    means = (mine_ref[...] + other_ref[...]) * (1.0 / full_width)
-    scale = lax.rsqrt(means[:, 0:1] + eps)
-    inner = means[:, 1:2]
+    scale = lax.rsqrt((sq0_ref[...] + sq1_ref[...])[:, 0:1] * (1.0 / full_width) + eps)
+    inner = (in0_ref[...] + in1_ref[...])[:, 0:1] * (1.0 / full_width)
     values = side_by_side(embedded_ref).astype(f32)
-    scaled = side_by_side(dnormed_ref).astype(f32) * gain_ref[...]
+    dnormed = side_by_side(kept_ref).astype(f32) + side_by_side(other_ref).astype(f32)
+    scaled = dnormed * gain_ref[...]
     dembed = scale * scaled - values * (scale * scale * scale * inner)
     out = dot(picks_ref[...], dembed.astype(bf16), 1, 0).astype(bf16)
     out_ref[...] = out.reshape(out_ref.shape)
 
 
-def dispatch(slot, dnormed, gain, embedded, mine, other, groups, cap, full_width, block):
+def dispatch(slot, kept, other, gain, embedded, sums, groups, cap, full_width, block):
     ngram, tokens = slot.shape
     width = embedded.shape[0] * SPAN
     slots = groups * ngram * cap
+    blocked = pl.BlockSpec((block // SPAN, tokens, SPAN), lambda j: (j, 0, 0))
+    total = pl.BlockSpec((tokens, LANES), lambda j: (0, 0))
     return pl.pallas_call(
         functools.partial(dispatch_body, full_width=full_width),
         grid=(width // block,),
         in_specs=[
             pl.BlockSpec((ngram, tokens), lambda j: (0, 0)),
-            pl.BlockSpec((block // SPAN, tokens, SPAN), lambda j: (j, 0, 0)),
+            blocked,
+            blocked,
             pl.BlockSpec((1, block), lambda j: (0, j)),
-            pl.BlockSpec((block // SPAN, tokens, SPAN), lambda j: (j, 0, 0)),
-            pl.BlockSpec((tokens, LANES), lambda j: (0, 0)),
-            pl.BlockSpec((tokens, LANES), lambda j: (0, 0)),
+            blocked,
+            total,
+            total,
+            total,
+            total,
         ],
         out_specs=pl.BlockSpec((groups, ngram, cap, block), lambda j: (0, 0, 0, j)),
         out_shape=jax.ShapeDtypeStruct((groups, ngram, cap, width), bf16),
         scratch_shapes=[pltpu.VMEM((slots, tokens), bf16)],
         name="dispatch",
-    )(slot, dnormed, gain, embedded, mine, other)
+    )(slot, kept, other, gain, embedded, *sums)
 
 
 def accumulate_body(asked_ref, arrived_ref, out_ref, picks_ref, *, cap):
@@ -299,27 +299,66 @@
     )(*cots, weight)
 
 
+def forward_body(*refs):
+    pieces, weight_ref, outs = refs[:4], refs[4], refs[5:]
+    for piece_ref, out_ref in zip(pieces, outs, strict=True):
+        out_ref[...] = dot(piece_ref[...], weight_ref[...], 1, 0).astype(out_ref.dtype)
+
+
+def forward(pieces, weight, block):
+    tokens, rows = pieces[0].shape
+    width = weight.shape[1]
+    return pl.pallas_call(
+        forward_body,
+        grid=(width // block,),
+        in_specs=[pl.BlockSpec((tokens, rows), lambda j: (0, 0)) for _ in pieces]
+        + [pl.BlockSpec((rows, block), lambda j: (0, j))],
+        out_specs=[pl.BlockSpec((tokens, block), lambda j: (0, j)) for _ in pieces],
+        out_shape=[
+            jax.ShapeDtypeStruct((tokens, width), bf16 if k else f32) for k in range(len(pieces))
+        ],
+        name="forward",
+    )(*pieces, weight)
+
+
 def feature_block(core, quarter, i):
     return jnp.where(core == 0, 4 * quarter + i, 4 * i + quarter)
 
 
-def arrange_body(place_ref, *refs):
+def arrange_body(place_ref, own_ref, theirs_ref, gain_ref, *refs):
     core, ring = place_ref[0], place_ref[1]
-    out_ref = refs[-1]
-    for k, ref in enumerate(refs[:-1]):
+    quarters, (kept_ref, given_ref, inner_ref) = refs[:-3], refs[-3:]
+    tokens = inner_ref.shape[0]
+    total = jnp.zeros((tokens, SPAN), f32)
+    for k, ref in enumerate(quarters):
         quarter = (ring + 4 - k) % 4
         for i in range(4):
-            out_ref[feature_block(core, quarter, i)] = ref[:, i * SPAN : (i + 1) * SPAN]
-
-
-def arrange(place, quarters):
+            at = feature_block(core, quarter, i)
+            here, ours = at % 8, at // 8 == core
+            piece = ref[:, i * SPAN : (i + 1) * SPAN]
+            values = jnp.where(ours, own_ref[here].astype(f32), theirs_ref[here].astype(f32))
+            total += values * (piece.astype(f32) * gain_ref[at])
+
+            @pl.when(ours)
+            def _():
+                kept_ref[here] = piece
+
+            @pl.when(jnp.logical_not(ours))
+            def _():
+                given_ref[here] = piece
+
+    inner_ref[...] = jnp.broadcast_to(jnp.sum(total, axis=1, keepdims=True), inner_ref.shape)
+
+
+def arrange(place, own, theirs, gain, quarters):
     tokens = quarters[0].shape[0]
+    half = jax.ShapeDtypeStruct((8, tokens, SPAN), bf16)
     return pl.pallas_call(
         arrange_body,
-        in_specs=[pl.BlockSpec(memory_space=pltpu.SMEM)] + [pl.BlockSpec(memory_space=pltpu.VMEM)] * 4,
-        out_shape=jax.ShapeDtypeStruct((16, tokens, SPAN), bf16),
+        in_specs=[pl.BlockSpec(memory_space=pltpu.SMEM)] + [pl.BlockSpec(memory_space=pltpu.VMEM)] * 7,
+        out_shape=(half, half, jax.ShapeDtypeStruct((tokens, LANES), f32)),
         name="arrange",
-    )(place, *quarters)
+    )(place, own, theirs, gain.reshape(16, 1, SPAN), *quarters)
 
 
 def normalize_body(place_ref, own_ref, theirs_ref, mine_ref, other_ref, gain_ref, *outs, full_width):
@@ -364,37 +403,34 @@
 
     blocks = [(proj_weight, 0)] + [(shifted(proj_weight, True, -k), k) for k in (1, 3, 2)]
     weight = joined(blocks, side, 0)
-    blocks = [(weight, 0)] + [(shifted_z(weight, -k), k) for k in (2, 1, 3)]
+    after, before = shifted_z(weight, -1), shifted_z(weight, 1)
+    opposite = [shifted_z(after[:2], -1), shifted_z(before[2:], 1)]
+    blocks = [(weight, 0), (after, 1), (before, 3), (jnp.concatenate(opposite), 2)]
     weight = joined(blocks, z, 1).reshape(-1, width)
-    cots = [cotangent] + [shifted(cotangent, False, -k) for k in (1, 2, 3)]
-
-    looked = lookup(asked, hash_tables, cap, block)
+    two, one, three = (shifted(cotangent, False, -k) for k in (2, 1, 3))
+    cots = [cotangent, one, two, three]
+
+    looked = lookup(asked, hash_tables, cap, 2 * block)
     fetched = exchange(looked)
 
     products = product(cots, weight, 256)
     quarters = [products[0]] + [shifted(products[k], False, k) for k in (1, 2, 3)]
     place = jnp.stack([half, ring]).astype(i32)
-    partial = arrange(place, quarters)
-    two = partial.shape[0] // 2
-    other = swapped(lax.dynamic_slice_in_dim(partial, (1 - half) * two, two))
-    kept = lax.dynamic_slice_in_dim(partial, half * two, two)
-    dnormed = (kept.astype(f32) + other.astype(f32)).astype(bf16)
-    embedded, sums = combine(slot, byte_ids, fetched, byte_table, dnormed, gain_half, block)
-    others = swapped(sums)
+    embedded, square = combine(slot, byte_ids, fetched, byte_table, block)
+    squares = (square, swapped(square))
     theirs = swapped(embedded)
-    sends = dispatch(
-        slot, dnormed, gain_half, embedded, sums, others, groups, cap, full_width, block
-    )
-
-    pieces = normalize(place, embedded, theirs, sums, others, gain, full_width)
+    pieces = normalize(place, embedded, theirs, *squares, gain, full_width)
     turned = [pieces[0]] + [shifted(pieces[k], False, k) for k in (1, 2, 3)]
+    kept, given, inner = arrange(place, embedded, theirs, gain, quarters)
+    other = swapped(given)
+    sums = (*squares, inner, swapped(inner))
+    sends = dispatch(slot, kept, other, gain_half, embedded, sums, groups, cap, full_width, block)
     arrived = exchange(sends)
 
-    projected = dot(turned[0], weight, 1, 0)
+    projected, *others = forward(turned, weight, block)
     for k in (2, 1, 3):
-        piece = dot(turned[k], weight, 1, 0).astype(bf16)
-        projected = projected + shifted(piece, False, -k).astype(f32)
-    table_grads = accumulate(asked, arrived, rows, block)
+        projected = projected + shifted(others[k - 1], False, -k).astype(f32)
+    table_grads = accumulate(asked, arrived, rows, 2 * block)
     return (projected.astype(bf16), table_grads)
 
 

time: 312 us -> 313 us (level)
  waiting for transfers between devices: 147 us -> 166 us
  matrix products: 15.2 us -> 0 us
  Pallas kernels: 50.7 us -> 57.8 us
  starting transfers between devices: 59.4 us -> 52.9 us
  blocking collectives: 21.2 us -> 16.9 us
    ppermute x15, waiting for transfers between devices: 84.9 us -> 141 us  [shifted(): return lax.ppermute(array, ('x', 'y', 'mp'), pairs)]
    ppermute x3 -> x4, waiting for transfers between devices: 57.3 us -> 23 us  [shifted_z(): return lax.ppermute(array, 'z', [(i, (i + by) % 4) for i in range(4)])]
    dot_general x4 -> x0, matrix products: 15.2 us -> none  [dot(): lax.dot_general(a, b, (((ca,), (cb,)), ((), ())), preferred_element_type=...]
    pallas_call x0 -> x1, Pallas kernels: none -> 7.74 us  [forward(): pl.pallas_call(forward_body, grid=(width // block,), in_specs=[pl.BlockSp...]
    all_to_all x1, blocking collectives: 21.2 us -> 16.9 us  [exchange(): return lax.all_to_all(array, AXES, split_axis=0, concat_axis=0, tiled=True)]
    all_to_all x2, starting transfers between devices: 24 us -> 20.6 us  [exchange(): return lax.all_to_all(array, AXES, split_axis=0, concat_axis=0, tiled=True)]
  transfers between devices with their start and end apart: 23 -> 25, of which waited for: 13 -> 13; matrix products, arithmetic and copies ran while one was open for 9% -> 5% of each run, Pallas kernels for 11% -> 8%
where the time goes in v2:
time: 313 us; the launch traced here: 312 us
  waiting for transfers between devices  166 us (53%)
  Pallas kernels  57.8 us (18%)
  starting transfers between devices  52.9 us (17%)
  blocking collectives  16.9 us (5%)
  local copies, waits for them, and re-layouts  11.4 us (4%)
  other arithmetic  6.16 us (2%)
    ppermute x15, waiting for transfers between devices, shifted(): return lax.ppermute(array, ('x', 'y', 'mp'), pairs)  141 us
    ppermute x15, starting transfers between devices, shifted(): return lax.ppermute(array, ('x', 'y', 'mp'), pairs)  27.6 us
    ppermute x4, waiting for transfers between devices, shifted_z(): return lax.ppermute(array, 'z', [(i, (i + by) % 4) for i in range(4)])  23 us
    all_to_all x2, starting transfers between devices, exchange(): return lax.all_to_all(array, AXES, split_axis=0, concat_axis=0, tiled=True)  20.6 us
    all_to_all x1, blocking collectives, exchange(): return lax.all_to_all(array, AXES, split_axis=0, concat_axis=0, tiled=True)  16.9 us
    pallas_call x1, Pallas kernels, accumulate(): pl.pallas_call(functools.partial(accumulate_body, cap=cap), grid=(ngram,...  9.8 us
    pallas_call x1, Pallas kernels, lookup(): pl.pallas_call(functools.partial(lookup_body, cap=cap), grid=(ngram, widt...  9.17 us
    pallas_call x1, Pallas kernels, product(): pl.pallas_call(product_body, grid=(rows // block,), in_specs=[pl.BlockSpe...  8.51 us
  transfers between devices with their start and end apart: 25, of which 13 were waited for; matrix products, arithmetic and copies ran while one was open for 5% of the time, Pallas kernels for 8%

profile of v2, /device:TPU:50, one launch (start us, length us, event | category | flops | bytes accessed | tf_op | source)
XLA Modules:
  0.0 311.8 jit_solution(6010368117776650652)
XLA Ops:
  0.6 1.8 route.1
  2.5 16.9 %all_to_all.15 = s32[64,1,128]{2,1,0:T(1,128)} all-to-all(s32[64,1,128]{2,1,0:T(1,128)} %bitcast.40), channel_id=1, replica_groups=mesh['x'=4,'y'=4,'z'=4,'mp'=2] {'x','y','z'}, dimensions={0} | all-to-all | bytes 65536 | tf_op jit(solution)/shard_map/all_to_all | solution.py:249
  19.4 9.2 %lookup.1 = bf16[64,2,8,2048]{3,2,1,0:T(8,128)(2,1)} custom-call(s32[64,128]{1,0:T(8,128)} %bitcast.35, bf16[2,1024,2048]{2,1,0:T(8,128)(2,1)} %table_ref.1), custom_call_target="tpu_custom_call" | custom-call | tf_op jit(solution)/shard_map/lookup/pallas_call | solution.py:83
  28.5 9.3 %all-to-all-start.1 = ((bf16[64,2,8,2048]{3,2,1,0:T(8,128)(2,1)}), bf16[64,2,8,2048]{3,2,1,0:T(8,128)(2,1)}, u32[]{:S(2)}, u32[]{:S(2)}) async-start(bf16[64,2,8,2048]{3,2,1,0:T(8,128)(2,1)} %lookup.1), calls=%async_computation.1 | async-start | bytes 8388608 | tf_op jit(solution)/shard_map/all_to_all | solution.py:249
  37.9 0.6 collective-permute-start.5
  38.5 1.5 collective-permute-start.6
  40.0 1.2 collective-permute-start.7
  41.2 0.1 broadcast_in_dim.34
  41.4 46.8 %collective-permute-done.5 = bf16[64,2048]{1,0:T(8,128)(2,1)S(1)} collective-permute-done((bf16[64,2048]{1,0:T(8,128)(2,1)S(1)}, bf16[64,2048]{1,0:T(8,128)(2,1)S(1)}, u32[]{:S(2)}, u32[]{:S(2)}) %collective-permute-start.5) | collective-permute-done | bytes 262176 | tf_op jit(solution)/shard_map/ppermute | solution.py:264
  88.2 3.5 %collective-permute-done.7 = bf16[64,2048]{1,0:T(8,128)(2,1)S(1)} collective-permute-done((bf16[64,2048]{1,0:T(8,128)(2,1)S(1)}, bf16[64,2048]{1,0:T(8,128)(2,1)S(1)}, u32[]{:S(2)}, u32[]{:S(2)}) %collective-permute-start.7) | collective-permute-done | bytes 262176 | tf_op jit(solution)/shard_map/ppermute | solution.py:264
  91.7 1.4 collective-permute-start.9
  93.1 0.7 collective-permute-start.8
  93.8 2.2 collective-permute-start.16
  96.0 2.2 collective-permute-start.17
  98.2 18.4 %collective-permute-done.9 = bf16[4,64,2048]{2,1,0:T(8,128)(2,1)S(1)} collective-permute-done((bf16[4,64,2048]{2,1,0:T(8,128)(2,1)S(1)}, bf16[4,64,2048]{2,1,0:T(8,128)(2,1)S(1)}, u32[]{:S(2)}, u32[]{:S(2)}) %collective-permute-start.9) | collective-permute-done | bytes 1048608 | tf_op jit(solution)/shard_map/ppermute | solution.py:268
  116.7 0.9 slice.9
  117.5 0.0 collective-permute-start.11
  117.5 2.5 broadcast_in_dim.33
  120.1 1.0 bitcast_dynamic-update-slice_fusion.2
  121.1 0.0 collective-permute-done.8
  121.1 0.9 slice.8
  122.0 2.0 collective-permute-start.10
  124.0 1.1 bitcast_dynamic-update-slice_fusion.1
  125.1 0.0 all-to-all-done.1.fetched_ref
  125.1 5.7 %combine.1 = (bf16[8,256,256]{2,1,0:T(8,128)(2,1)}, f32[256,128]{1,0:T(8,128)}) custom-call(s32[2,256]{1,0:T(2,128)} %get-tuple-element.21.slot_ref, s32[1,256]{1,0:T(1,128)} %bitcast.42, bf16[64,2,8,2048]{3,2,1,0:T(8,128)(2,1)} %all-to-all-done.1.fetched_ref, bf16[256,2048]{1,0:T(8,128)(2,1)} %bytes_ref.1), custom_call_target="tpu_custom_call" | custom-call | tf_op jit(solution)/shard_map/combine/pallas_call | solution.py:139
  130.7 1.6 collective-permute-done.11
  132.4 1.0 bitcast_dynamic-update-slice_fusion
  133.4 2.9 collective-permute-done.10
  136.3 2.3 fusion
  138.6 8.5 %product.1 = (bf16[256,1024]{1,0:T(8,128)(2,1)}, bf16[256,1024]{1,0:T(8,128)(2,1)}, bf16[256,1024]{1,0:T(8,128)(2,1)}, bf16[256,1024]{1,0:T(8,128)(2,1)}) custom-call(bf16[256,2048]{1,0:T(8,128)(2,1)} %refs_0_.1, bf16[256,2048]{1,0:T(8,128)(2,1)} %collective-permute-done.15.refs_1_, bf16[256,2048]{1,0:T(8,128)(2,1)} %collective-permute-done.16.refs_2_, ...), custom_call_target="tpu_custom_call" | custom-call | tf_op jit(solution)/shard_map/product/pallas_call | solution.py:291
  147.2 2.4 collective-permute-start.18
  149.5 2.5 collective-permute-start.19
  152.0 2.5 collective-permute-start.20
  154.6 0.7 pad_add_fusion.place_ref
  155.2 6.9 %collective-permute-done.18.refs_1_ = bf16[256,1024]{1,0:T(8,128)(2,1)S(1)} collective-permute-done((bf16[256,1024]{1,0:T(8,128)(2,1)}, bf16[256,1024]{1,0:T(8,128)(2,1)S(1)}, u32[]{:S(2)}, u32[]{:S(2)}) %collective-permute-start.18) | collective-permute-done | bytes 524320 | tf_op jit(solution)/shard_map/ppermute | solution.py:264
  162.2 3.9 %collective-permute-done.20.refs_3_ = bf16[256,1024]{1,0:T(8,128)(2,1)S(1)} collective-permute-done((bf16[256,1024]{1,0:T(8,128)(2,1)}, bf16[256,1024]{1,0:T(8,128)(2,1)S(1)}, u32[]{:S(2)}, u32[]{:S(2)}) %collective-permute-start.20) | collective-permute-done | bytes 524320 | tf_op jit(solution)/shard_map/ppermute | solution.py:264
  166.1 0.8 copy-done.6
  166.8 0.4 copy-done
  167.2 5.5 %arrange.1 = (bf16[8,256,256]{2,1,0:T(8,128)(2,1)}, bf16[8,256,256]{2,1,0:T(8,128)(2,1)}, f32[256,128]{1,0:T(8,128)}) custom-call(s32[2]{0:T(128)} %pad_add_fusion.place_ref, bf16[8,256,256]{2,1,0:T(8,128)(2,1)} %get-tuple-element.23.own_ref.embedded_ref, bf16[8,256,256]{2,1,0:T(8,128)(2,1)} %copy-done, f32[16,1,256]{2,1,0:T(1,128)} %bitcast.37, ...), custom_call_target="tpu_custom_call" | custom-call | tf_op jit(solution)/shard_map/arrange/pallas_call | solution.py:356
  172.8 0.5 collective-permute-start.1
  173.3 0.1 collective-permute-start.22
  173.4 0.6 dynamic_slice.3
  174.0 1.9 collective-permute-done.1.other_ref.sq1_ref
  175.8 0.2 collective-permute-done.22.in1_ref
  176.0 0.5 copy-done.3
  176.5 0.2 copy-done.11
  176.7 0.4 copy-done.1
  177.0 5.8 %dispatch.1 = bf16[64,2,8,2048]{3,2,1,0:T(8,128)(2,1)} custom-call(s32[2,256]{1,0:T(2,128)} %get-tuple-element.21.slot_ref, bf16[8,256,256]{2,1,0:T(8,128)(2,1)} %get-tuple-element.37.kept_ref, bf16[8,256,256]{2,1,0:T(8,128)(2,1)} %copy-done.1, f32[1,2048]{1,0:T(1,128)} %bitcast.39, bf16[8,256,256]{2,1,0:T(8,128)(2,1)} %get-tuple-element.23.own_ref.embedded_ref, ...), custom_call_target="tpu_custom_call" | custom-call | tf_op jit(solution)/shard_map/dispatch/pallas_call | solution.py:190
  182.9 11.3 %all-to-all-start.2 = ((bf16[64,2,8,2048]{3,2,1,0:T(8,128)(2,1)}), bf16[64,2,8,2048]{3,2,1,0:T(8,128)(2,1)}, u32[]{:S(2)}, u32[]{:S(2)}) async-start(bf16[64,2,8,2048]{3,2,1,0:T(8,128)(2,1)} %dispatch.1), calls=%async_computation.2 | async-start | bytes 8388608 | tf_op jit(solution)/shard_map/all_to_all | solution.py:249
  194.2 3.7 %normalize.1 = (bf16[256,1024]{1,0:T(8,128)(2,1)}, bf16[256,1024]{1,0:T(8,128)(2,1)}, bf16[256,1024]{1,0:T(8,128)(2,1)}, bf16[256,1024]{1,0:T(8,128)(2,1)}) custom-call(s32[2]{0:T(128)} %pad_add_fusion.place_ref, bf16[8,256,256]{2,1,0:T(8,128)(2,1)} %get-tuple-element.23.own_ref.embedded_ref, bf16[8,256,256]{2,1,0:T(8,128)(2,1)} %copy-done, ...), custom_call_target="tpu_custom_call" | custom-call | tf_op jit(solution)/shard_map/normalize/pallas_call | solution.py:378
  197.9 1.6 collective-permute-start.2
  199.5 1.0 collective-permute-start.3
  200.5 2.3 collective-permute-start.4
  202.8 46.3 %collective-permute-done.2.refs_1_ = bf16[256,1024]{1,0:T(8,128)(2,1)S(1)} collective-permute-done((bf16[256,1024]{1,0:T(8,128)(2,1)}, bf16[256,1024]{1,0:T(8,128)(2,1)S(1)}, u32[]{:S(2)}, u32[]{:S(2)}) %collective-permute-start.2) | collective-permute-done | bytes 524320 | tf_op jit(solution)/shard_map/ppermute | solution.py:264
  249.1 8.8 %collective-permute-done.3.refs_2_ = bf16[256,1024]{1,0:T(8,128)(2,1)S(1)} collective-permute-done((bf16[256,1024]{1,0:T(8,128)(2,1)}, bf16[256,1024]{1,0:T(8,128)(2,1)S(1)}, u32[]{:S(2)}, u32[]{:S(2)}) %collective-permute-start.3) | collective-permute-done | bytes 524320 | tf_op jit(solution)/shard_map/ppermute | solution.py:264
  257.9 0.8 copy-done.8
  258.6 0.2 copy-done.9
  258.8 7.7 %forward.1 = (f32[256,2048]{1,0:T(8,128)}, bf16[256,2048]{1,0:T(8,128)(2,1)}, bf16[256,2048]{1,0:T(8,128)(2,1)}, bf16[256,2048]{1,0:T(8,128)(2,1)}) custom-call(bf16[256,1024]{1,0:T(8,128)(2,1)} %get-tuple-element.25.refs_0_, bf16[256,1024]{1,0:T(8,128)(2,1)} %copy-done.7, bf16[256,1024]{1,0:T(8,128)(2,1)} %copy-done.8, bf16[256,1024]{1,0:T(8,128)(2,1)} %copy-done.9, ...), custom_call_target="tpu_custom_call" | custom-call | tf_op jit(solution)/shard_map/forward/pallas_call | solution.py:311
  266.5 6.0 %collective-permute-start.14 = (bf16[256,2048]{1,0:T(8,128)(2,1)}, bf16[256,2048]{1,0:T(8,128)(2,1)S(1)}, u32[]{:S(2)}, u32[]{:S(2)}) collective-permute-start(bf16[256,2048]{1,0:T(8,128)(2,1)} %get-tuple-element.32), channel_id=1, source_target_pairs={{0,32},{1,9},{8,40},{9,17},{16,48},{17,25},{24,56},{25,1},{32,64},... | collective-permute-start | bytes 3145736 | tf_op jit(solution)/shard_map/ppermute | solution.py:264
  272.6 1.5 collective-permute-start.12
  274.1 22.3 %collective-permute-done.14 = bf16[256,2048]{1,0:T(8,128)(2,1)S(1)} collective-permute-done((bf16[256,2048]{1,0:T(8,128)(2,1)}, bf16[256,2048]{1,0:T(8,128)(2,1)S(1)}, u32[]{:S(2)}, u32[]{:S(2)}) %collective-permute-start.14) | collective-permute-done | bytes 1048608 | tf_op jit(solution)/shard_map/ppermute | solution.py:264
  296.4 2.4 collective-permute-done.13
  298.8 3.2 %add_convert_fusion = bf16[256,2048]{1,0:T(8,128)(2,1)} fusion(bf16[256,2048]{1,0:T(8,128)(2,1)S(1)} %collective-permute-done.14, bf16[256,2048]{1,0:T(8,128)(2,1)S(1)} %collective-permute-done.13, f32[256,2048]{1,0:T(8,128)} %get-tuple-element.29, bf16[256,2048]{1,0:T(8,128)(2,1)S(1)} %collective-permute-done.12), kind=kLoop, calls=%fused_computation | loop fusion | flops 3670016 | bytes 6291456 | tf_op jit(solution)/shard_map/convert_element_type | solution.py:434
  302.0 9.8 %accumulate.1 = bf16[2,1024,2048]{2,1,0:T(8,128)(2,1)} custom-call(s32[64,128]{1,0:T(8,128)} %bitcast.36, bf16[64,2,8,2048]{3,2,1,0:T(8,128)(2,1)} %all-to-all-done.2.arrived_ref), custom_call_target="tpu_custom_call" | custom-call | tf_op jit(solution)/shard_map/accumulate/pallas_call | solution.py:234
  (37 shorter events, 0.2 us)
Async XLA Ops:
  28.5 9.3 %copy-start.10 = (bf16[64,2048]{1,0:T(8,128)(2,1)S(1)}, bf16[64,2048]{1,0:T(8,128)(2,1)}, u32[]{:S(2)}) copy-start(bf16[64,2048]{1,0:T(8,128)(2,1)} %param.14) | copy-start | bytes 786436
  28.5 96.5 %all-to-all-start.1 = ((bf16[64,2,8,2048]{3,2,1,0:T(8,128)(2,1)}), bf16[64,2,8,2048]{3,2,1,0:T(8,128)(2,1)}, u32[]{:S(2)}, u32[]{:S(2)}) async-start(bf16[64,2,8,2048]{3,2,1,0:T(8,128)(2,1)} %lookup.1), calls=%async_computation.1 | async-start | bytes 8388608 | tf_op jit(solution)/shard_map/all_to_all | solution.py:249
  37.9 50.3 %collective-permute-start.5 = (bf16[64,2048]{1,0:T(8,128)(2,1)S(1)}, bf16[64,2048]{1,0:T(8,128)(2,1)S(1)}, u32[]{:S(2)}, u32[]{:S(2)}) collective-permute-start(bf16[64,2048]{1,0:T(8,128)(2,1)S(1)} %copy-done.10), channel_id=1, source_target_pairs={{0,24},{1,97},{8,0},{9,105},{16,8},{17,113},{24,16},{25,121},{32,5... | collective-permute-start | bytes 786440 | tf_op jit(solution)/shard_map/ppermute | solution.py:264
  38.5 49.7 %collective-permute-start.6 = (bf16[64,2048]{1,0:T(8,128)(2,1)S(1)}, bf16[64,2048]{1,0:T(8,128)(2,1)S(1)}, u32[]{:S(2)}, u32[]{:S(2)}) collective-permute-start(bf16[64,2048]{1,0:T(8,128)(2,1)S(1)} %copy-done.10), channel_id=1, source_target_pairs={{0,8},{1,33},{8,16},{9,41},{16,24},{17,49},{24,0},{25,57},{32,40},... | collective-permute-start | bytes 786440 | tf_op jit(solution)/shard_map/ppermute | solution.py:264
  40.0 51.7 %collective-permute-start.7 = (bf16[64,2048]{1,0:T(8,128)(2,1)S(1)}, bf16[64,2048]{1,0:T(8,128)(2,1)S(1)}, u32[]{:S(2)}, u32[]{:S(2)}) collective-permute-start(bf16[64,2048]{1,0:T(8,128)(2,1)S(1)} %copy-done.10), channel_id=1, source_target_pairs={{0,16},{1,65},{8,24},{9,73},{16,0},{17,81},{24,8},{25,89},{32,48},... | collective-permute-start | bytes 786440 | tf_op jit(solution)/shard_map/ppermute | solution.py:264
  91.7 25.0 %collective-permute-start.9 = (bf16[4,64,2048]{2,1,0:T(8,128)(2,1)S(1)}, bf16[4,64,2048]{2,1,0:T(8,128)(2,1)S(1)}, u32[]{:S(2)}, u32[]{:S(2)}) collective-permute-start(bf16[4,64,2048]{2,1,0:T(8,128)(2,1)S(1)} %bitcast_dynamic-update-slice_fusion.3), channel_id=1, source_target_pairs={{0,2},{2,4},{4,6},{6,0},{1,3},{3,5},{5,7},{7,1},{8,10},{10,12},{12... | collective-permute-start | bytes 3145736 | tf_op jit(solution)/shard_map/ppermute | solution.py:268
  93.1 28.0 %collective-permute-start.8 = (bf16[4,64,2048]{2,1,0:T(8,128)(2,1)S(1)}, bf16[4,64,2048]{2,1,0:T(8,128)(2,1)S(1)}, u32[]{:S(2)}, u32[]{:S(2)}) collective-permute-start(bf16[4,64,2048]{2,1,0:T(8,128)(2,1)S(1)} %bitcast_dynamic-update-slice_fusion.3), channel_id=1, source_target_pairs={{0,6},{2,0},{4,2},{6,4},{1,7},{3,1},{5,3},{7,5},{8,14},{10,8},{12,... | collective-permute-start | bytes 3145736 | tf_op jit(solution)/shard_map/ppermute | solution.py:268
  93.8 44.8 %collective-permute-start.15 = (bf16[256,2048]{1,0:T(8,128)(2,1)}, bf16[256,2048]{1,0:T(8,128)(2,1)}, u32[]{:S(2)}, u32[]{:S(2)}) collective-permute-start(bf16[256,2048]{1,0:T(8,128)(2,1)} %refs_0_.1), channel_id=1, source_target_pairs={{0,96},{1,25},{8,104},{9,1},{16,112},{17,9},{24,120},{25,17},{32,0... | collective-permute-start | bytes 3145736 | tf_op jit(solution)/shard_map/ppermute | solution.py:264
  93.8 44.8 %collective-permute-start.16 = (bf16[256,2048]{1,0:T(8,128)(2,1)}, bf16[256,2048]{1,0:T(8,128)(2,1)}, u32[]{:S(2)}, u32[]{:S(2)}) collective-permute-start(bf16[256,2048]{1,0:T(8,128)(2,1)} %refs_0_.1), channel_id=1, source_target_pairs={{0,64},{1,17},{8,72},{9,25},{16,80},{17,1},{24,88},{25,9},{32,96},... | collective-permute-start | bytes 3145736 | tf_op jit(solution)/shard_map/ppermute | solution.py:264
  96.0 42.6 %collective-permute-start.17 = (bf16[256,2048]{1,0:T(8,128)(2,1)}, bf16[256,2048]{1,0:T(8,128)(2,1)}, u32[]{:S(2)}, u32[]{:S(2)}) collective-permute-start(bf16[256,2048]{1,0:T(8,128)(2,1)} %refs_0_.1), channel_id=1, source_target_pairs={{0,32},{1,9},{8,40},{9,17},{16,48},{17,25},{24,56},{25,1},{32,64},... | collective-permute-start | bytes 3145736 | tf_op jit(solution)/shard_map/ppermute | solution.py:264
  117.5 14.8 %collective-permute-start.11 = (bf16[2,64,2048]{2,1,0:T(8,128)(2,1)}, bf16[2,64,2048]{2,1,0:T(8,128)(2,1)}, u32[]{:S(2)}, u32[]{:S(2)}) collective-permute-start(bf16[2,64,2048]{2,1,0:T(8,128)(2,1)} %slice.9), channel_id=1, source_target_pairs={{0,2},{2,4},{4,6},{6,0},{1,3},{3,5},{5,7},{7,1},{8,10},{10,12},{12... | collective-permute-start | bytes 1572872 | tf_op jit(solution)/shard_map/ppermute | solution.py:268
  122.0 14.4 %collective-permute-start.10 = (bf16[2,64,2048]{2,1,0:T(8,128)(2,1)}, bf16[2,64,2048]{2,1,0:T(8,128)(2,1)}, u32[]{:S(2)}, u32[]{:S(2)}) collective-permute-start(bf16[2,64,2048]{2,1,0:T(8,128)(2,1)} %slice.8), channel_id=1, source_target_pairs={{0,6},{2,0},{4,2},{6,4},{1,7},{3,1},{5,3},{7,5},{8,14},{10,8},{12,... | collective-permute-start | bytes 1572872 | tf_op jit(solution)/shard_map/ppermute | solution.py:268
  132.4 33.7 %collective-permute-start = (bf16[8,256,256]{2,1,0:T(8,128)(2,1)}, bf16[8,256,256]{2,1,0:T(8,128)(2,1)S(1)}, u32[]{:S(2)}, u32[]{:S(2)}) collective-permute-start(bf16[8,256,256]{2,1,0:T(8,128)(2,1)} %get-tuple-element.23.own_ref.embedded_ref), channel_id=1, source_target_pairs={{0,1},{1,0},{2,3},{3,2},{4,5},{5,4},{6,7},{7,6},{8,9},{9,8},{10,11... | collective-permute-start | bytes 3145736 | tf_op jit(solution)/shard_map/ppermute | solution.py:253
  147.1 25.6 %copy-start.2 = (f32[256,128]{1,0:T(8,128)S(1)}, f32[256,128]{1,0:T(8,128)}, u32[]{:S(2)}) copy-start(f32[256,128]{1,0:T(8,128)} %get-tuple-element.24.mine_ref.sq0_ref) | copy-start | bytes 393220
  147.1 26.2 %copy-start.12 = (f32[4096]{0:T(1024)S(1)}, f32[4096]{0:T(1024)}, u32[]{:S(2)}) copy-start(f32[4096]{0:T(1024)} %param.13) | copy-start | bytes 49156
  147.2 15.0 %collective-permute-start.18 = (bf16[256,1024]{1,0:T(8,128)(2,1)}, bf16[256,1024]{1,0:T(8,128)(2,1)S(1)}, u32[]{:S(2)}, u32[]{:S(2)}) collective-permute-start(bf16[256,1024]{1,0:T(8,128)(2,1)} %get-tuple-element.34), channel_id=1, source_target_pairs={{0,32},{1,9},{8,40},{9,17},{16,48},{17,25},{24,56},{25,1},{32,64},... | collective-permute-start | bytes 1572872 | tf_op jit(solution)/shard_map/ppermute | solution.py:264
  149.5 12.6 %collective-permute-start.19 = (bf16[256,1024]{1,0:T(8,128)(2,1)}, bf16[256,1024]{1,0:T(8,128)(2,1)S(1)}, u32[]{:S(2)}, u32[]{:S(2)}) collective-permute-start(bf16[256,1024]{1,0:T(8,128)(2,1)} %get-tuple-element.35), channel_id=1, source_target_pairs={{0,64},{1,17},{8,72},{9,25},{16,80},{17,1},{24,88},{25,9},{32,96},... | collective-permute-start | bytes 1572872 | tf_op jit(solution)/shard_map/ppermute | solution.py:264
  152.0 14.0 %collective-permute-start.20 = (bf16[256,1024]{1,0:T(8,128)(2,1)}, bf16[256,1024]{1,0:T(8,128)(2,1)S(1)}, u32[]{:S(2)}, u32[]{:S(2)}) collective-permute-start(bf16[256,1024]{1,0:T(8,128)(2,1)} %get-tuple-element.36), channel_id=1, source_target_pairs={{0,96},{1,25},{8,104},{9,1},{16,112},{17,9},{24,120},{25,17},{32,0... | collective-permute-start | bytes 1572872 | tf_op jit(solution)/shard_map/ppermute | solution.py:264
  162.1 3.9 %copy-start.4 = (bf16[256,1024]{1,0:T(8,128)(2,1)}, bf16[256,1024]{1,0:T(8,128)(2,1)S(1)}, u32[]{:S(2)}) copy-start(bf16[256,1024]{1,0:T(8,128)(2,1)S(1)} %collective-permute-done.18.refs_1_) | copy-start | bytes 1572868
  162.2 3.9 %copy-start.5 = (bf16[256,1024]{1,0:T(8,128)(2,1)}, bf16[256,1024]{1,0:T(8,128)(2,1)S(1)}, u32[]{:S(2)}) copy-start(bf16[256,1024]{1,0:T(8,128)(2,1)S(1)} %collective-permute-done.19.refs_2_) | copy-start | bytes 1572868
  166.0 0.8 copy-start.6
  166.0 1.2 copy-start
  172.8 3.3 %collective-permute-start.21 = (bf16[8,256,256]{2,1,0:T(8,128)(2,1)}, bf16[8,256,256]{2,1,0:T(8,128)(2,1)S(1)}, u32[]{:S(2)}, u32[]{:S(2)}) collective-permute-start(bf16[8,256,256]{2,1,0:T(8,128)(2,1)} %get-tuple-element.38), channel_id=1, source_target_pairs={{0,1},{1,0},{2,3},{3,2},{4,5},{5,4},{6,7},{7,6},{8,9},{9,8},{10,11... | collective-permute-start | bytes 3145736 | tf_op jit(solution)/shard_map/ppermute | solution.py:253
  172.8 3.0 collective-permute-start.1
  173.3 2.7 collective-permute-start.22
  175.8 0.6 copy-start.3
  176.0 0.6 copy-start.11
  176.0 1.0 copy-start.1
  182.9 119.2 %all-to-all-start.2 = ((bf16[64,2,8,2048]{3,2,1,0:T(8,128)(2,1)}), bf16[64,2,8,2048]{3,2,1,0:T(8,128)(2,1)}, u32[]{:S(2)}, u32[]{:S(2)}) async-start(bf16[64,2,8,2048]{3,2,1,0:T(8,128)(2,1)} %dispatch.1), calls=%async_computation.2 | async-start | bytes 8388608 | tf_op jit(solution)/shard_map/all_to_all | solution.py:249
  197.9 51.2 %collective-permute-start.2 = (bf16[256,1024]{1,0:T(8,128)(2,1)}, bf16[256,1024]{1,0:T(8,128)(2,1)S(1)}, u32[]{:S(2)}, u32[]{:S(2)}) collective-permute-start(bf16[256,1024]{1,0:T(8,128)(2,1)} %get-tuple-element.26), channel_id=1, source_target_pairs={{0,32},{1,9},{8,40},{9,17},{16,48},{17,25},{24,56},{25,1},{32,64},... | collective-permute-start | bytes 1572872 | tf_op jit(solution)/shard_map/ppermute | solution.py:264
  199.5 58.4 %collective-permute-start.3 = (bf16[256,1024]{1,0:T(8,128)(2,1)}, bf16[256,1024]{1,0:T(8,128)(2,1)S(1)}, u32[]{:S(2)}, u32[]{:S(2)}) collective-permute-start(bf16[256,1024]{1,0:T(8,128)(2,1)} %get-tuple-element.27), channel_id=1, source_target_pairs={{0,64},{1,17},{8,72},{9,25},{16,80},{17,1},{24,88},{25,9},{32,96},... | collective-permute-start | bytes 1572872 | tf_op jit(solution)/shard_map/ppermute | solution.py:264
  200.5 57.4 %collective-permute-start.4 = (bf16[256,1024]{1,0:T(8,128)(2,1)}, bf16[256,1024]{1,0:T(8,128)(2,1)S(1)}, u32[]{:S(2)}, u32[]{:S(2)}) collective-permute-start(bf16[256,1024]{1,0:T(8,128)(2,1)} %get-tuple-element.28), channel_id=1, source_target_pairs={{0,96},{1,25},{8,104},{9,1},{16,112},{17,9},{24,120},{25,17},{32,0... | collective-permute-start | bytes 1572872 | tf_op jit(solution)/shard_map/ppermute | solution.py:264
  249.1 8.8 %copy-start.7 = (bf16[256,1024]{1,0:T(8,128)(2,1)}, bf16[256,1024]{1,0:T(8,128)(2,1)S(1)}, u32[]{:S(2)}) copy-start(bf16[256,1024]{1,0:T(8,128)(2,1)S(1)} %collective-permute-done.2.refs_1_) | copy-start | bytes 1572868
  257.8 0.8 copy-start.8
  257.8 1.0 copy-start.9
  266.5 29.9 %collective-permute-start.14 = (bf16[256,2048]{1,0:T(8,128)(2,1)}, bf16[256,2048]{1,0:T(8,128)(2,1)S(1)}, u32[]{:S(2)}, u32[]{:S(2)}) collective-permute-start(bf16[256,2048]{1,0:T(8,128)(2,1)} %get-tuple-element.32), channel_id=1, source_target_pairs={{0,32},{1,9},{8,40},{9,17},{16,48},{17,25},{24,56},{25,1},{32,64},... | collective-permute-start | bytes 3145736 | tf_op jit(solution)/shard_map/ppermute | solution.py:264
  272.6 26.2 %collective-permute-start.13 = (bf16[256,2048]{1,0:T(8,128)(2,1)}, bf16[256,2048]{1,0:T(8,128)(2,1)S(1)}, u32[]{:S(2)}, u32[]{:S(2)}) collective-permute-start(bf16[256,2048]{1,0:T(8,128)(2,1)} %get-tuple-element.31), channel_id=1, source_target_pairs={{0,96},{1,25},{8,104},{9,1},{16,112},{17,9},{24,120},{25,17},{32,0... | collective-permute-start | bytes 3145736 | tf_op jit(solution)/shard_map/ppermute | solution.py:264
  272.6 26.2 %collective-permute-start.12 = (bf16[256,2048]{1,0:T(8,128)(2,1)}, bf16[256,2048]{1,0:T(8,128)(2,1)S(1)}, u32[]{:S(2)}, u32[]{:S(2)}) collective-permute-start(bf16[256,2048]{1,0:T(8,128)(2,1)} %get-tuple-element.30), channel_id=1, source_target_pairs={{0,64},{1,17},{8,72},{9,25},{16,80},{17,1},{24,88},{25,9},{32,96},... | collective-permute-start | bytes 3145736 | tf_op jit(solution)/shard_map/ppermute | solution.py:264

commit v3 on v2

--- a/solution.py
+++ b/solution.py
@@ -300,12 +300,13 @@
 
 
 def forward_body(*refs):
-    pieces, weight_ref, outs = refs[:4], refs[4], refs[5:]
+    count = len(refs) // 2
+    pieces, weight_ref, outs = refs[:count], refs[count], refs[count + 1 :]
     for piece_ref, out_ref in zip(pieces, outs, strict=True):
         out_ref[...] = dot(piece_ref[...], weight_ref[...], 1, 0).astype(out_ref.dtype)
 
 
-def forward(pieces, weight, block):
+def forward(pieces, weight, block, types):
     tokens, rows = pieces[0].shape
     width = weight.shape[1]
     return pl.pallas_call(
@@ -314,9 +315,7 @@
         in_specs=[pl.BlockSpec((tokens, rows), lambda j: (0, 0)) for _ in pieces]
         + [pl.BlockSpec((rows, block), lambda j: (0, j))],
         out_specs=[pl.BlockSpec((tokens, block), lambda j: (0, j)) for _ in pieces],
-        out_shape=[
-            jax.ShapeDtypeStruct((tokens, width), bf16 if k else f32) for k in range(len(pieces))
-        ],
+        out_shape=[jax.ShapeDtypeStruct((tokens, width), kind) for kind in types],
         name="forward",
     )(*pieces, weight)
 
@@ -325,19 +324,23 @@
     return jnp.where(core == 0, 4 * quarter + i, 4 * i + quarter)
 
 
-def arrange_body(place_ref, own_ref, theirs_ref, gain_ref, *refs):
+def settle_body(place_ref, own_ref, theirs_ref, gain_ref, mine_ref, other_ref, *refs, full_width):
     core, ring = place_ref[0], place_ref[1]
-    quarters, (kept_ref, given_ref, inner_ref) = refs[:-3], refs[-3:]
+    quarters, (kept_ref, given_ref, inner_ref), pieces = refs[:4], refs[4:7], refs[7:]
     tokens = inner_ref.shape[0]
+    scale = lax.rsqrt((mine_ref[...] + other_ref[...])[:, 0:1] * (1.0 / full_width) + eps)
     total = jnp.zeros((tokens, SPAN), f32)
     for k, ref in enumerate(quarters):
         quarter = (ring + 4 - k) % 4
         for i in range(4):
             at = feature_block(core, quarter, i)
             here, ours = at % 8, at // 8 == core
-            piece = ref[:, i * SPAN : (i + 1) * SPAN]
+            lanes = slice(i * SPAN, (i + 1) * SPAN)
+            piece = ref[:, lanes]
+            gain = gain_ref[at]
             values = jnp.where(ours, own_ref[here].astype(f32), theirs_ref[here].astype(f32))
-            total += values * (piece.astype(f32) * gain_ref[at])
+            total += values * (piece.astype(f32) * gain)
+            pieces[(4 - k) % 4][:, lanes] = (values * scale * gain).astype(bf16)
 
             @pl.when(ours)
             def _():
@@ -350,37 +353,34 @@
     inner_ref[...] = jnp.broadcast_to(jnp.sum(total, axis=1, keepdims=True), inner_ref.shape)
 
 
-def arrange(place, own, theirs, gain, quarters):
-    tokens = quarters[0].shape[0]
+def settle(place, own, theirs, gain, squares, quarters, full_width, block):
+    tokens = own.shape[1]
+    blocked = pl.BlockSpec((8, block, SPAN), lambda j: (0, j, 0))
+    flat = pl.BlockSpec((block, 4 * SPAN), lambda j: (j, 0))
+    total = pl.BlockSpec((block, LANES), lambda j: (j, 0))
     half = jax.ShapeDtypeStruct((8, tokens, SPAN), bf16)
-    return pl.pallas_call(
-        arrange_body,
-        in_specs=[pl.BlockSpec(memory_space=pltpu.SMEM)] + [pl.BlockSpec(memory_space=pltpu.VMEM)] * 7,
-        out_shape=(half, half, jax.ShapeDtypeStruct((tokens, LANES), f32)),
-        name="arrange",
-    )(place, own, theirs, gain.reshape(16, 1, SPAN), *quarters)
-
-
-def normalize_body(place_ref, own_ref, theirs_ref, mine_ref, other_ref, gain_ref, *outs, full_width):
-    core, ring = place_ref[0], place_ref[1]
-    means = (mine_ref[...] + other_ref[...])[:, 0:1] * (1.0 / full_width)
-    scale = lax.rsqrt(means + eps)
-    for k, out_ref in enumerate(outs):
-        quarter = (ring + k) % 4
-        for i in range(4):
-            at = feature_block(core, quarter, i)
-            piece = jnp.where(at // 8 == core, own_ref[at % 8].astype(f32), theirs_ref[at % 8].astype(f32))
-            out_ref[:, i * SPAN : (i + 1) * SPAN] = (piece * scale * gain_ref[at]).astype(bf16)
-
-
-def normalize(place, own, theirs, mine, other, gain, full_width):
-    tokens = own.shape[1]
-    return pl.pallas_call(
-        functools.partial(normalize_body, full_width=full_width),
-        in_specs=[pl.BlockSpec(memory_space=pltpu.SMEM)] + [pl.BlockSpec(memory_space=pltpu.VMEM)] * 5,
-        out_shape=[jax.ShapeDtypeStruct((tokens, 4 * SPAN), bf16)] * 4,
-        name="normalize",
-    )(place, own, theirs, mine, other, gain.reshape(16, 1, SPAN))
+    out = pl.pallas_call(
+        functools.partial(settle_body, full_width=full_width),
+        grid=(tokens // block,),
+        in_specs=[
+            pl.BlockSpec(memory_space=pltpu.SMEM),
+            blocked,
+            blocked,
+            pl.BlockSpec((16, 1, SPAN), lambda j: (0, 0, 0)),
+            total,
+            total,
+            *[flat] * 4,
+        ],
+        out_specs=[blocked, blocked, total, *[flat] * 4],
+        out_shape=[
+            half,
+            half,
+            jax.ShapeDtypeStruct((tokens, LANES), f32),
+            *[jax.ShapeDtypeStruct((tokens, 4 * SPAN), bf16)] * 4,
+        ],
+        name="settle",
+    )(place, own, theirs, gain.reshape(16, 1, SPAN), *squares, *quarters)
+    return out[0], out[1], out[2], out[3:]
 
 
 def on_device(
@@ -419,17 +419,20 @@
     embedded, square = combine(slot, byte_ids, fetched, byte_table, block)
     squares = (square, swapped(square))
     theirs = swapped(embedded)
-    pieces = normalize(place, embedded, theirs, *squares, gain, full_width)
-    turned = [pieces[0]] + [shifted(pieces[k], False, k) for k in (1, 2, 3)]
-    kept, given, inner = arrange(place, embedded, theirs, gain, quarters)
+    kept, given, inner, pieces = settle(
+        place, embedded, theirs, gain, squares, quarters, full_width, tokens // 4
+    )
     other = swapped(given)
     sums = (*squares, inner, swapped(inner))
+    across, near, last = (shifted(pieces[k], False, k) for k in (2, 1, 3))
     sends = dispatch(slot, kept, other, gain_half, embedded, sums, groups, cap, full_width, block)
     arrived = exchange(sends)
 
-    projected, *others = forward(turned, weight, block)
-    for k in (2, 1, 3):
-        projected = projected + shifted(others[k - 1], False, -k).astype(f32)
+    returned = [shifted(forward([across], weight, block, [bf16])[0], False, -2)]
+    projected, *others = forward([pieces[0], near, last], weight, block, [f32, bf16, bf16])
+    returned += [shifted(other, False, -k) for other, k in zip(others, (1, 3), strict=True)]
+    for other in returned:
+        projected = projected + other.astype(f32)
     table_grads = accumulate(asked, arrived, rows, 2 * block)
     return (projected.astype(bf16), table_grads)
 

time: 313 us -> 306 us (0.978)
  waiting for transfers between devices: 166 us -> 156 us
    ppermute x15, waiting for transfers between devices: 141 us -> 131 us  [shifted(): return lax.ppermute(array, ('x', 'y', 'mp'), pairs)]
    pallas_call x1 -> x2, Pallas kernels: 7.74 us -> 11.8 us  [forward(): pl.pallas_call(forward_body, grid=(width // block,), in_specs=[pl.BlockSp...]
    pallas_call x2 -> x1, Pallas kernels: 9.27 us -> 5.99 us  [settle(): pl.pallas_call(functools.partial(settle_body, full_width=full_width), gri...]
  transfers between devices with their start and end apart: 25 -> 25, of which waited for: 13 -> 11; matrix products, arithmetic and copies ran while one was open for 5% -> 5% of each run, Pallas kernels for 8% -> 9%
where the time goes in v3:
time: 306 us; the launch traced here: 305 us
  waiting for transfers between devices  156 us (51%)
  Pallas kernels  58.7 us (19%)
  starting transfers between devices  55.4 us (18%)
  blocking collectives  16.9 us (6%)
  local copies, waits for them, and re-layouts  11.5 us (4%)
  other arithmetic  5.67 us (2%)
    ppermute x15, waiting for transfers between devices, shifted(): return lax.ppermute(array, ('x', 'y', 'mp'), pairs)  131 us
    ppermute x15, starting transfers between devices, shifted(): return lax.ppermute(array, ('x', 'y', 'mp'), pairs)  30 us
    ppermute x4, waiting for transfers between devices, shifted_z(): return lax.ppermute(array, 'z', [(i, (i + by) % 4) for i in range(4)])  23 us
    all_to_all x2, starting transfers between devices, exchange(): return lax.all_to_all(array, AXES, split_axis=0, concat_axis=0, tiled=True)  20.8 us
    all_to_all x1, blocking collectives, exchange(): return lax.all_to_all(array, AXES, split_axis=0, concat_axis=0, tiled=True)  16.9 us
    pallas_call x2, Pallas kernels, forward(): pl.pallas_call(forward_body, grid=(width // block,), in_specs=[pl.BlockSp...  11.8 us
    pallas_call x1, Pallas kernels, accumulate(): pl.pallas_call(functools.partial(accumulate_body, cap=cap), grid=(ngram,...  9.8 us
    pallas_call x1, Pallas kernels, lookup(): pl.pallas_call(functools.partial(lookup_body, cap=cap), grid=(ngram, widt...  9.17 us
  transfers between devices with their start and end apart: 25, of which 11 were waited for; matrix products, arithmetic and copies ran while one was open for 5% of the time, Pallas kernels for 9%

profile of v3, /device:TPU:50, one launch (start us, length us, event | category | flops | bytes accessed | tf_op | source)
XLA Modules:
  0.0 305.3 jit_solution(17688211952933670239)
XLA Ops:
  0.6 1.8 route.1
  2.5 16.9 %all_to_all.15 = s32[64,1,128]{2,1,0:T(1,128)} all-to-all(s32[64,1,128]{2,1,0:T(1,128)} %bitcast.39), channel_id=1, replica_groups=mesh['x'=4,'y'=4,'z'=4,'mp'=2] {'x','y','z'}, dimensions={0} | all-to-all | bytes 65536 | tf_op jit(solution)/shard_map/all_to_all | solution.py:249
  19.4 9.2 %lookup.1 = bf16[64,2,8,2048]{3,2,1,0:T(8,128)(2,1)} custom-call(s32[64,128]{1,0:T(8,128)} %bitcast.35, bf16[2,1024,2048]{2,1,0:T(8,128)(2,1)} %table_ref.1), custom_call_target="tpu_custom_call" | custom-call | tf_op jit(solution)/shard_map/lookup/pallas_call | solution.py:83
  28.5 9.3 %all-to-all-start.1 = ((bf16[64,2,8,2048]{3,2,1,0:T(8,128)(2,1)}), bf16[64,2,8,2048]{3,2,1,0:T(8,128)(2,1)}, u32[]{:S(2)}, u32[]{:S(2)}) async-start(bf16[64,2,8,2048]{3,2,1,0:T(8,128)(2,1)} %lookup.1), calls=%async_computation.1 | async-start | bytes 8388608 | tf_op jit(solution)/shard_map/all_to_all | solution.py:249
  37.9 0.6 collective-permute-start.5
  38.5 1.5 collective-permute-start.6
  40.0 1.2 collective-permute-start.7
  41.2 0.1 broadcast_in_dim.34
  41.4 46.8 %collective-permute-done.5 = bf16[64,2048]{1,0:T(8,128)(2,1)S(1)} collective-permute-done((bf16[64,2048]{1,0:T(8,128)(2,1)S(1)}, bf16[64,2048]{1,0:T(8,128)(2,1)S(1)}, u32[]{:S(2)}, u32[]{:S(2)}) %collective-permute-start.5) | collective-permute-done | bytes 262176 | tf_op jit(solution)/shard_map/ppermute | solution.py:264
  88.2 0.0 collective-permute-done.6
  88.2 3.5 %collective-permute-done.7 = bf16[64,2048]{1,0:T(8,128)(2,1)S(1)} collective-permute-done((bf16[64,2048]{1,0:T(8,128)(2,1)S(1)}, bf16[64,2048]{1,0:T(8,128)(2,1)S(1)}, u32[]{:S(2)}, u32[]{:S(2)}) %collective-permute-start.7) | collective-permute-done | bytes 262176 | tf_op jit(solution)/shard_map/ppermute | solution.py:264
  91.7 1.4 collective-permute-start.9
  93.1 0.7 collective-permute-start.8
  93.8 2.2 collective-permute-start.3
  96.0 2.2 collective-permute-start.4
  98.2 18.4 %collective-permute-done.9 = bf16[4,64,2048]{2,1,0:T(8,128)(2,1)S(1)} collective-permute-done((bf16[4,64,2048]{2,1,0:T(8,128)(2,1)S(1)}, bf16[4,64,2048]{2,1,0:T(8,128)(2,1)S(1)}, u32[]{:S(2)}, u32[]{:S(2)}) %collective-permute-start.9) | collective-permute-done | bytes 1048608 | tf_op jit(solution)/shard_map/ppermute | solution.py:268
  116.7 0.9 slice.9
  117.5 2.5 broadcast_in_dim.33
  120.1 1.1 bitcast_dynamic-update-slice_fusion.2
  121.1 0.0 collective-permute-done.8
  121.1 0.8 slice.8
  122.0 2.0 collective-permute-start.10
  124.0 1.1 bitcast_dynamic-update-slice_fusion.1
  125.1 5.7 %combine.1 = (bf16[8,256,256]{2,1,0:T(8,128)(2,1)}, f32[256,128]{1,0:T(8,128)}) custom-call(s32[2,256]{1,0:T(2,128)} %get-tuple-element.20.slot_ref, s32[1,256]{1,0:T(1,128)} %bitcast.41, bf16[64,2,8,2048]{3,2,1,0:T(8,128)(2,1)} %all-to-all-done.1.fetched_ref, bf16[256,2048]{1,0:T(8,128)(2,1)} %bytes_ref.1), custom_call_target="tpu_custom_call" | custom-call | tf_op jit(solution)/shard_map/combine/pallas_call | solution.py:139
  130.8 1.6 collective-permute-done.11
  132.4 0.0 collective-permute-start
  132.4 1.1 bitcast_dynamic-update-slice_fusion
  133.4 2.9 collective-permute-done.10
  136.4 2.3 fusion
  138.7 8.6 %product.1 = (bf16[256,1024]{1,0:T(8,128)(2,1)}, bf16[256,1024]{1,0:T(8,128)(2,1)}, bf16[256,1024]{1,0:T(8,128)(2,1)}, bf16[256,1024]{1,0:T(8,128)(2,1)}) custom-call(bf16[256,2048]{1,0:T(8,128)(2,1)} %refs_0_.1, bf16[256,2048]{1,0:T(8,128)(2,1)} %collective-permute-done.2.refs_1_, bf16[256,2048]{1,0:T(8,128)(2,1)} %collective-permute-done.3.refs_2_, ...), custom_call_target="tpu_custom_call" | custom-call | tf_op jit(solution)/shard_map/product/pallas_call | solution.py:291
  147.2 2.3 collective-permute-start.12
  149.6 2.5 collective-permute-start.13
  152.1 2.5 collective-permute-start.14
  154.6 0.0 collective-permute-start.1
  154.6 0.6 pad_add_fusion.place_ref
  155.2 7.0 %collective-permute-done.12.refs_1_ = bf16[256,1024]{1,0:T(8,128)(2,1)S(1)} collective-permute-done((bf16[256,1024]{1,0:T(8,128)(2,1)}, bf16[256,1024]{1,0:T(8,128)(2,1)S(1)}, u32[]{:S(2)}, u32[]{:S(2)}) %collective-permute-start.12) | collective-permute-done | bytes 524320 | tf_op jit(solution)/shard_map/ppermute | solution.py:264
  162.2 3.9 %collective-permute-done.14.refs_3_ = bf16[256,1024]{1,0:T(8,128)(2,1)S(1)} collective-permute-done((bf16[256,1024]{1,0:T(8,128)(2,1)}, bf16[256,1024]{1,0:T(8,128)(2,1)S(1)}, u32[]{:S(2)}, u32[]{:S(2)}) %collective-permute-start.14) | collective-permute-done | bytes 524320 | tf_op jit(solution)/shard_map/ppermute | solution.py:264
  166.1 0.0 copy-start.1
  166.1 0.8 copy-done.7
  166.9 0.0 copy-done.4
  166.9 0.3 copy-done.1
  167.3 6.0 %settle.1 = (bf16[8,256,256]{2,1,0:T(8,128)(2,1)}, bf16[8,256,256]{2,1,0:T(8,128)(2,1)}, f32[256,128]{1,0:T(8,128)}, bf16[256,1024]{1,0:T(8,128)(2,1)}, bf16[256...) custom-call(s32[2]{0:T(128)} %pad_add_fusion.place_ref, ...), custom_call_target="tpu_custom_call" | custom-call | tf_op jit(solution)/shard_map/settle/pallas_call | solution.py:362
  173.3 0.1 collective-permute-start.21
  173.4 0.5 collective-permute-start.22
  173.9 0.6 dynamic_slice.3
  174.5 1.9 collective-permute-done.22.in1_ref
  176.4 0.6 copy-done.11
  177.1 0.4 copy-done.2
  177.4 5.8 %dispatch.1 = bf16[64,2,8,2048]{3,2,1,0:T(8,128)(2,1)} custom-call(s32[2,256]{1,0:T(2,128)} %get-tuple-element.20.slot_ref, bf16[8,256,256]{2,1,0:T(8,128)(2,1)} %get-tuple-element.35.kept_ref, bf16[8,256,256]{2,1,0:T(8,128)(2,1)} %copy-done.2, f32[1,2048]{1,0:T(1,128)} %bitcast.38, bf16[8,256,256]{2,1,0:T(8,128)(2,1)} %get-tuple-element.22.own_ref.embedded_ref, ...), custom_call_target="tpu_custom_call" | custom-call | tf_op jit(solution)/shard_map/dispatch/pallas_call | solution.py:190
  183.3 11.4 %all-to-all-start.2 = ((bf16[64,2,8,2048]{3,2,1,0:T(8,128)(2,1)}), bf16[64,2,8,2048]{3,2,1,0:T(8,128)(2,1)}, u32[]{:S(2)}, u32[]{:S(2)}) async-start(bf16[64,2,8,2048]{3,2,1,0:T(8,128)(2,1)} %dispatch.1), calls=%async_computation.2 | async-start | bytes 8388608 | tf_op jit(solution)/shard_map/all_to_all | solution.py:249
  194.7 1.6 collective-permute-start.15
  196.4 0.5 collective-permute-start.16
  196.8 2.3 collective-permute-start.17
  199.1 50.5 %collective-permute-done.15.refs_1_ = bf16[256,1024]{1,0:T(8,128)(2,1)S(1)} collective-permute-done((bf16[256,1024]{1,0:T(8,128)(2,1)S(1)}, bf16[256,1024]{1,0:T(8,128)(2,1)S(1)}, u32[]{:S(2)}, u32[]{:S(2)}) %collective-permute-start.15) | collective-permute-done | bytes 524320 | tf_op jit(solution)/shard_map/ppermute | solution.py:264
  249.6 0.8 copy-done.8
  250.4 0.2 copy-done.9
  250.6 6.8 %forward.2 = (f32[256,2048]{1,0:T(8,128)}, bf16[256,2048]{1,0:T(8,128)(2,1)}, bf16[256,2048]{1,0:T(8,128)(2,1)}) custom-call(bf16[256,1024]{1,0:T(8,128)(2,1)} %get-tuple-element.28.refs_0_, bf16[256,1024]{1,0:T(8,128)(2,1)} %copy-done.8, bf16[256,1024]{1,0:T(8,128)(2,1)} %copy-done.9, bf16[1024,2048]{1,0:T(8,128)(2,1)} %bitcast.19.refs_4_.refs_3_.refs_1_), custom_call_target="tpu_custom_call" | custom-call | tf_op jit(solution)/shard_map/forward/pallas_call | solution.py:312
  257.4 8.9 %collective-permute-start.20 = (bf16[256,2048]{1,0:T(8,128)(2,1)}, bf16[256,2048]{1,0:T(8,128)(2,1)S(1)}, u32[]{:S(2)}, u32[]{:S(2)}) collective-permute-start(bf16[256,2048]{1,0:T(8,128)(2,1)} %get-tuple-element.34), channel_id=1, source_target_pairs={{0,32},{1,9},{8,40},{9,17},{16,48},{17,25},{24,56},{25,1},{32,64},... | collective-permute-start | bytes 3145736 | tf_op jit(solution)/shard_map/ppermute | solution.py:264
  266.4 5.0 %forward.3 = bf16[256,2048]{1,0:T(8,128)(2,1)} custom-call(bf16[256,1024]{1,0:T(8,128)(2,1)} %collective-permute-done.17.refs_0_, bf16[1024,2048]{1,0:T(8,128)(2,1)} %bitcast.19.refs_4_.refs_3_.refs_1_), custom_call_target="tpu_custom_call" | custom-call | tf_op jit(solution)/shard_map/forward/pallas_call | solution.py:312
  271.4 1.5 collective-permute-start.18
  272.9 17.3 %collective-permute-done.20 = bf16[256,2048]{1,0:T(8,128)(2,1)S(1)} collective-permute-done((bf16[256,2048]{1,0:T(8,128)(2,1)}, bf16[256,2048]{1,0:T(8,128)(2,1)S(1)}, u32[]{:S(2)}, u32[]{:S(2)}) %collective-permute-start.20) | collective-permute-done | bytes 1048608 | tf_op jit(solution)/shard_map/ppermute | solution.py:264
  290.2 2.5 collective-permute-done.19
  292.7 2.8 add_convert_fusion
  295.5 9.8 %accumulate.1 = bf16[2,1024,2048]{2,1,0:T(8,128)(2,1)} custom-call(s32[64,128]{1,0:T(8,128)} %bitcast.36, bf16[64,2,8,2048]{3,2,1,0:T(8,128)(2,1)} %all-to-all-done.2.arrived_ref), custom_call_target="tpu_custom_call" | custom-call | tf_op jit(solution)/shard_map/accumulate/pallas_call | solution.py:234
  (41 shorter events, 0.2 us)
Async XLA Ops:
  28.5 9.3 %copy-start.10 = (bf16[64,2048]{1,0:T(8,128)(2,1)S(1)}, bf16[64,2048]{1,0:T(8,128)(2,1)}, u32[]{:S(2)}) copy-start(bf16[64,2048]{1,0:T(8,128)(2,1)} %param.14) | copy-start | bytes 786436
  28.5 96.6 %all-to-all-start.1 = ((bf16[64,2,8,2048]{3,2,1,0:T(8,128)(2,1)}), bf16[64,2,8,2048]{3,2,1,0:T(8,128)(2,1)}, u32[]{:S(2)}, u32[]{:S(2)}) async-start(bf16[64,2,8,2048]{3,2,1,0:T(8,128)(2,1)} %lookup.1), calls=%async_computation.1 | async-start | bytes 8388608 | tf_op jit(solution)/shard_map/all_to_all | solution.py:249
  37.9 50.3 %collective-permute-start.5 = (bf16[64,2048]{1,0:T(8,128)(2,1)S(1)}, bf16[64,2048]{1,0:T(8,128)(2,1)S(1)}, u32[]{:S(2)}, u32[]{:S(2)}) collective-permute-start(bf16[64,2048]{1,0:T(8,128)(2,1)S(1)} %copy-done.10), channel_id=1, source_target_pairs={{0,24},{1,97},{8,0},{9,105},{16,8},{17,113},{24,16},{25,121},{32,5... | collective-permute-start | bytes 786440 | tf_op jit(solution)/shard_map/ppermute | solution.py:264
  38.5 49.7 %collective-permute-start.6 = (bf16[64,2048]{1,0:T(8,128)(2,1)S(1)}, bf16[64,2048]{1,0:T(8,128)(2,1)S(1)}, u32[]{:S(2)}, u32[]{:S(2)}) collective-permute-start(bf16[64,2048]{1,0:T(8,128)(2,1)S(1)} %copy-done.10), channel_id=1, source_target_pairs={{0,8},{1,33},{8,16},{9,41},{16,24},{17,49},{24,0},{25,57},{32,40},... | collective-permute-start | bytes 786440 | tf_op jit(solution)/shard_map/ppermute | solution.py:264
  40.0 51.7 %collective-permute-start.7 = (bf16[64,2048]{1,0:T(8,128)(2,1)S(1)}, bf16[64,2048]{1,0:T(8,128)(2,1)S(1)}, u32[]{:S(2)}, u32[]{:S(2)}) collective-permute-start(bf16[64,2048]{1,0:T(8,128)(2,1)S(1)} %copy-done.10), channel_id=1, source_target_pairs={{0,16},{1,65},{8,24},{9,73},{16,0},{17,81},{24,8},{25,89},{32,48},... | collective-permute-start | bytes 786440 | tf_op jit(solution)/shard_map/ppermute | solution.py:264
  91.7 25.0 %collective-permute-start.9 = (bf16[4,64,2048]{2,1,0:T(8,128)(2,1)S(1)}, bf16[4,64,2048]{2,1,0:T(8,128)(2,1)S(1)}, u32[]{:S(2)}, u32[]{:S(2)}) collective-permute-start(bf16[4,64,2048]{2,1,0:T(8,128)(2,1)S(1)} %bitcast_dynamic-update-slice_fusion.3), channel_id=1, source_target_pairs={{0,2},{2,4},{4,6},{6,0},{1,3},{3,5},{5,7},{7,1},{8,10},{10,12},{12... | collective-permute-start | bytes 3145736 | tf_op jit(solution)/shard_map/ppermute | solution.py:268
  93.1 28.0 %collective-permute-start.8 = (bf16[4,64,2048]{2,1,0:T(8,128)(2,1)S(1)}, bf16[4,64,2048]{2,1,0:T(8,128)(2,1)S(1)}, u32[]{:S(2)}, u32[]{:S(2)}) collective-permute-start(bf16[4,64,2048]{2,1,0:T(8,128)(2,1)S(1)} %bitcast_dynamic-update-slice_fusion.3), channel_id=1, source_target_pairs={{0,6},{2,0},{4,2},{6,4},{1,7},{3,1},{5,3},{7,5},{8,14},{10,8},{12,... | collective-permute-start | bytes 3145736 | tf_op jit(solution)/shard_map/ppermute | solution.py:268
  93.8 44.9 %collective-permute-start.2 = (bf16[256,2048]{1,0:T(8,128)(2,1)}, bf16[256,2048]{1,0:T(8,128)(2,1)}, u32[]{:S(2)}, u32[]{:S(2)}) collective-permute-start(bf16[256,2048]{1,0:T(8,128)(2,1)} %refs_0_.1), channel_id=1, source_target_pairs={{0,96},{1,25},{8,104},{9,1},{16,112},{17,9},{24,120},{25,17},{32,0... | collective-permute-start | bytes 3145736 | tf_op jit(solution)/shard_map/ppermute | solution.py:264
  93.8 44.9 %collective-permute-start.3 = (bf16[256,2048]{1,0:T(8,128)(2,1)}, bf16[256,2048]{1,0:T(8,128)(2,1)}, u32[]{:S(2)}, u32[]{:S(2)}) collective-permute-start(bf16[256,2048]{1,0:T(8,128)(2,1)} %refs_0_.1), channel_id=1, source_target_pairs={{0,64},{1,17},{8,72},{9,25},{16,80},{17,1},{24,88},{25,9},{32,96},... | collective-permute-start | bytes 3145736 | tf_op jit(solution)/shard_map/ppermute | solution.py:264
  96.0 42.6 %collective-permute-start.4 = (bf16[256,2048]{1,0:T(8,128)(2,1)}, bf16[256,2048]{1,0:T(8,128)(2,1)}, u32[]{:S(2)}, u32[]{:S(2)}) collective-permute-start(bf16[256,2048]{1,0:T(8,128)(2,1)} %refs_0_.1), channel_id=1, source_target_pairs={{0,32},{1,9},{8,40},{9,17},{16,48},{17,25},{24,56},{25,1},{32,64},... | collective-permute-start | bytes 3145736 | tf_op jit(solution)/shard_map/ppermute | solution.py:264
  117.5 14.8 %collective-permute-start.11 = (bf16[2,64,2048]{2,1,0:T(8,128)(2,1)}, bf16[2,64,2048]{2,1,0:T(8,128)(2,1)}, u32[]{:S(2)}, u32[]{:S(2)}) collective-permute-start(bf16[2,64,2048]{2,1,0:T(8,128)(2,1)} %slice.9), channel_id=1, source_target_pairs={{0,2},{2,4},{4,6},{6,0},{1,3},{3,5},{5,7},{7,1},{8,10},{10,12},{12... | collective-permute-start | bytes 1572872 | tf_op jit(solution)/shard_map/ppermute | solution.py:268
  122.0 14.4 %collective-permute-start.10 = (bf16[2,64,2048]{2,1,0:T(8,128)(2,1)}, bf16[2,64,2048]{2,1,0:T(8,128)(2,1)}, u32[]{:S(2)}, u32[]{:S(2)}) collective-permute-start(bf16[2,64,2048]{2,1,0:T(8,128)(2,1)} %slice.8), channel_id=1, source_target_pairs={{0,6},{2,0},{4,2},{6,4},{1,7},{3,1},{5,3},{7,5},{8,14},{10,8},{12,... | collective-permute-start | bytes 1572872 | tf_op jit(solution)/shard_map/ppermute | solution.py:268
  132.4 33.7 %collective-permute-start = (bf16[8,256,256]{2,1,0:T(8,128)(2,1)}, bf16[8,256,256]{2,1,0:T(8,128)(2,1)S(1)}, u32[]{:S(2)}, u32[]{:S(2)}) collective-permute-start(bf16[8,256,256]{2,1,0:T(8,128)(2,1)} %get-tuple-element.22.own_ref.embedded_ref), channel_id=1, source_target_pairs={{0,1},{1,0},{2,3},{3,2},{4,5},{5,4},{6,7},{7,6},{8,9},{9,8},{10,11... | collective-permute-start | bytes 3145736 | tf_op jit(solution)/shard_map/ppermute | solution.py:253
  138.7 15.9 %copy-start.3 = (f32[256,128]{1,0:T(8,128)S(1)}, f32[256,128]{1,0:T(8,128)}, u32[]{:S(2)}) copy-start(f32[256,128]{1,0:T(8,128)} %get-tuple-element.23.mine_ref.sq0_ref) | copy-start | bytes 393220
  147.2 26.6 %copy-start.12 = (f32[4096]{0:T(1024)S(1)}, f32[4096]{0:T(1024)}, u32[]{:S(2)}) copy-start(f32[4096]{0:T(1024)} %param.13) | copy-start | bytes 49156
  147.2 15.0 %collective-permute-start.12 = (bf16[256,1024]{1,0:T(8,128)(2,1)}, bf16[256,1024]{1,0:T(8,128)(2,1)S(1)}, u32[]{:S(2)}, u32[]{:S(2)}) collective-permute-start(bf16[256,1024]{1,0:T(8,128)(2,1)} %get-tuple-element.25), channel_id=1, source_target_pairs={{0,32},{1,9},{8,40},{9,17},{16,48},{17,25},{24,56},{25,1},{32,64},... | collective-permute-start | bytes 1572872 | tf_op jit(solution)/shard_map/ppermute | solution.py:264
  149.6 12.6 %collective-permute-start.13 = (bf16[256,1024]{1,0:T(8,128)(2,1)}, bf16[256,1024]{1,0:T(8,128)(2,1)S(1)}, u32[]{:S(2)}, u32[]{:S(2)}) collective-permute-start(bf16[256,1024]{1,0:T(8,128)(2,1)} %get-tuple-element.26), channel_id=1, source_target_pairs={{0,64},{1,17},{8,72},{9,25},{16,80},{17,1},{24,88},{25,9},{32,96},... | collective-permute-start | bytes 1572872 | tf_op jit(solution)/shard_map/ppermute | solution.py:264
  152.1 14.0 %collective-permute-start.14 = (bf16[256,1024]{1,0:T(8,128)(2,1)}, bf16[256,1024]{1,0:T(8,128)(2,1)S(1)}, u32[]{:S(2)}, u32[]{:S(2)}) collective-permute-start(bf16[256,1024]{1,0:T(8,128)(2,1)} %get-tuple-element.27), channel_id=1, source_target_pairs={{0,96},{1,25},{8,104},{9,1},{16,112},{17,9},{24,120},{25,17},{32,0... | collective-permute-start | bytes 1572872 | tf_op jit(solution)/shard_map/ppermute | solution.py:264
  154.6 11.5 %collective-permute-start.1 = (f32[256,128]{1,0:T(8,128)S(1)}, f32[256,128]{1,0:T(8,128)S(1)}, u32[]{:S(2)}, u32[]{:S(2)}) collective-permute-start(f32[256,128]{1,0:T(8,128)S(1)} %copy-done.3), channel_id=1, source_target_pairs={{0,1},{1,0},{2,3},{3,2},{4,5},{5,4},{6,7},{7,6},{8,9},{9,8},{10,11... | collective-permute-start | bytes 393224 | tf_op jit(solution)/shard_map/ppermute | solution.py:253
  162.2 3.9 %copy-start.5 = (bf16[256,1024]{1,0:T(8,128)(2,1)}, bf16[256,1024]{1,0:T(8,128)(2,1)S(1)}, u32[]{:S(2)}) copy-start(bf16[256,1024]{1,0:T(8,128)(2,1)S(1)} %collective-permute-done.12.refs_1_) | copy-start | bytes 1572868
  162.2 3.9 %copy-start.6 = (bf16[256,1024]{1,0:T(8,128)(2,1)}, bf16[256,1024]{1,0:T(8,128)(2,1)S(1)}, u32[]{:S(2)}) copy-start(bf16[256,1024]{1,0:T(8,128)(2,1)S(1)} %collective-permute-done.13.refs_2_) | copy-start | bytes 1572868
  166.1 0.8 copy-start.7
  166.1 0.8 copy-start.4
  166.1 1.2 copy-start.1
  173.3 3.1 %collective-permute-start.21 = (bf16[8,256,256]{2,1,0:T(8,128)(2,1)}, bf16[8,256,256]{2,1,0:T(8,128)(2,1)S(1)}, u32[]{:S(2)}, u32[]{:S(2)}) collective-permute-start(bf16[8,256,256]{2,1,0:T(8,128)(2,1)} %get-tuple-element.36), channel_id=1, source_target_pairs={{0,1},{1,0},{2,3},{3,2},{4,5},{5,4},{6,7},{7,6},{8,9},{9,8},{10,11... | collective-permute-start | bytes 3145736 | tf_op jit(solution)/shard_map/ppermute | solution.py:253
  173.4 3.0 collective-permute-start.22
  176.4 0.6 copy-start.11
  176.4 1.0 copy-start.2
  183.3 11.5 %copy-start.14 = (bf16[256,1024]{1,0:T(8,128)(2,1)S(1)}, bf16[256,1024]{1,0:T(8,128)(2,1)}, u32[]{:S(2)}) copy-start(bf16[256,1024]{1,0:T(8,128)(2,1)} %get-tuple-element.29) | copy-start | bytes 1572868
  183.3 13.1 %copy-start.13 = (bf16[256,1024]{1,0:T(8,128)(2,1)S(1)}, bf16[256,1024]{1,0:T(8,128)(2,1)}, u32[]{:S(2)}) copy-start(bf16[256,1024]{1,0:T(8,128)(2,1)} %get-tuple-element.30) | copy-start | bytes 1572868
  183.3 112.3 %all-to-all-start.2 = ((bf16[64,2,8,2048]{3,2,1,0:T(8,128)(2,1)}), bf16[64,2,8,2048]{3,2,1,0:T(8,128)(2,1)}, u32[]{:S(2)}, u32[]{:S(2)}) async-start(bf16[64,2,8,2048]{3,2,1,0:T(8,128)(2,1)} %dispatch.1), calls=%async_computation.2 | async-start | bytes 8388608 | tf_op jit(solution)/shard_map/all_to_all | solution.py:249
  194.7 54.9 %collective-permute-start.15 = (bf16[256,1024]{1,0:T(8,128)(2,1)S(1)}, bf16[256,1024]{1,0:T(8,128)(2,1)S(1)}, u32[]{:S(2)}, u32[]{:S(2)}) collective-permute-start(bf16[256,1024]{1,0:T(8,128)(2,1)S(1)} %copy-done.14), channel_id=1, source_target_pairs={{0,32},{1,9},{8,40},{9,17},{16,48},{17,25},{24,56},{25,1},{32,64},... | collective-permute-start | bytes 1572872 | tf_op jit(solution)/shard_map/ppermute | solution.py:264
  196.4 53.3 %collective-permute-start.16 = (bf16[256,1024]{1,0:T(8,128)(2,1)S(1)}, bf16[256,1024]{1,0:T(8,128)(2,1)S(1)}, u32[]{:S(2)}, u32[]{:S(2)}) collective-permute-start(bf16[256,1024]{1,0:T(8,128)(2,1)S(1)} %copy-done.13), channel_id=1, source_target_pairs={{0,96},{1,25},{8,104},{9,1},{16,112},{17,9},{24,120},{25,17},{32,0... | collective-permute-start | bytes 1572872 | tf_op jit(solution)/shard_map/ppermute | solution.py:264
  196.8 69.5 %collective-permute-start.17 = (bf16[256,1024]{1,0:T(8,128)(2,1)}, bf16[256,1024]{1,0:T(8,128)(2,1)}, u32[]{:S(2)}, u32[]{:S(2)}) collective-permute-start(bf16[256,1024]{1,0:T(8,128)(2,1)} %get-tuple-element.32), channel_id=1, source_target_pairs={{0,64},{1,17},{8,72},{9,25},{16,80},{17,1},{24,88},{25,9},{32,96},... | collective-permute-start | bytes 1572872 | tf_op jit(solution)/shard_map/ppermute | solution.py:264
  249.6 0.8 copy-start.8
  249.6 1.0 copy-start.9
  257.4 35.3 %copy-start = (f32[256,2048]{1,0:T(8,128)S(1)}, f32[256,2048]{1,0:T(8,128)}, u32[]{:S(2)}) copy-start(f32[256,2048]{1,0:T(8,128)} %get-tuple-element.31) | copy-start | bytes 6291460
  257.4 32.8 %collective-permute-start.20 = (bf16[256,2048]{1,0:T(8,128)(2,1)}, bf16[256,2048]{1,0:T(8,128)(2,1)S(1)}, u32[]{:S(2)}, u32[]{:S(2)}) collective-permute-start(bf16[256,2048]{1,0:T(8,128)(2,1)} %get-tuple-element.34), channel_id=1, source_target_pairs={{0,32},{1,9},{8,40},{9,17},{16,48},{17,25},{24,56},{25,1},{32,64},... | collective-permute-start | bytes 3145736 | tf_op jit(solution)/shard_map/ppermute | solution.py:264
  266.4 26.4 %collective-permute-start.19 = (bf16[256,2048]{1,0:T(8,128)(2,1)}, bf16[256,2048]{1,0:T(8,128)(2,1)}, u32[]{:S(2)}, u32[]{:S(2)}) collective-permute-start(bf16[256,2048]{1,0:T(8,128)(2,1)} %get-tuple-element.33), channel_id=1, source_target_pairs={{0,96},{1,25},{8,104},{9,1},{16,112},{17,9},{24,120},{25,17},{32,0... | collective-permute-start | bytes 3145736 | tf_op jit(solution)/shard_map/ppermute | solution.py:264
  271.4 21.3 %collective-permute-start.18 = (bf16[256,2048]{1,0:T(8,128)(2,1)}, bf16[256,2048]{1,0:T(8,128)(2,1)S(1)}, u32[]{:S(2)}, u32[]{:S(2)}) collective-permute-start(bf16[256,2048]{1,0:T(8,128)(2,1)} %forward.3), channel_id=1, source_target_pairs={{0,64},{1,17},{8,72},{9,25},{16,80},{17,1},{24,88},{25,9},{32,96},... | collective-permute-start | bytes 3145736 | tf_op jit(solution)/shard_map/ppermute | solution.py:264

commit v4 on v3

--- a/solution.py
+++ b/solution.py
@@ -416,19 +416,19 @@
     products = product(cots, weight, 256)
     quarters = [products[0]] + [shifted(products[k], False, k) for k in (1, 2, 3)]
     place = jnp.stack([half, ring]).astype(i32)
-    embedded, square = combine(slot, byte_ids, fetched, byte_table, block)
+    embedded, square = combine(slot, byte_ids, fetched, byte_table, 2 * block)
     squares = (square, swapped(square))
     theirs = swapped(embedded)
     kept, given, inner, pieces = settle(
-        place, embedded, theirs, gain, squares, quarters, full_width, tokens // 4
+        place, embedded, theirs, gain, squares, quarters, full_width, tokens // 2
     )
     other = swapped(given)
     sums = (*squares, inner, swapped(inner))
     across, near, last = (shifted(pieces[k], False, k) for k in (2, 1, 3))
-    sends = dispatch(slot, kept, other, gain_half, embedded, sums, groups, cap, full_width, block)
+    sends = dispatch(slot, kept, other, gain_half, embedded, sums, groups, cap, full_width, 2 * block)
     arrived = exchange(sends)
 
-    returned = [shifted(forward([across], weight, block, [bf16])[0], False, -2)]
+    returned = [shifted(forward([across], weight, 2 * block, [bf16])[0], False, -2)]
     projected, *others = forward([pieces[0], near, last], weight, block, [f32, bf16, bf16])
     returned += [shifted(other, False, -k) for other, k in zip(others, (1, 3), strict=True)]
     for other in returned:

time: 306 us -> 304 us (level)
  Pallas kernels: 58.7 us -> 55 us
  transfers between devices with their start and end apart: 25 -> 25, of which waited for: 11 -> 11; matrix products, arithmetic and copies ran while one was open for 5% -> 5% of each run, Pallas kernels for 9% -> 8%
where the time goes in v4:
time: 304 us
  waiting for transfers between devices  158 us (52%)
  starting transfers between devices  55.5 us (18%)
  Pallas kernels  55 us (18%)
  blocking collectives  16.9 us (6%)
  local copies, waits for them, and re-layouts  11.5 us (4%)
  other arithmetic  5.67 us (2%)
    ppermute x15, waiting for transfers between devices, shifted(): return lax.ppermute(array, ('x', 'y', 'mp'), pairs)  133 us
    ppermute x15, starting transfers between devices, shifted(): return lax.ppermute(array, ('x', 'y', 'mp'), pairs)  30 us
    ppermute x4, waiting for transfers between devices, shifted_z(): return lax.ppermute(array, 'z', [(i, (i + by) % 4) for i in range(4)])  23.8 us
    all_to_all x2, starting transfers between devices, exchange(): return lax.all_to_all(array, AXES, split_axis=0, concat_axis=0, tiled=True)  20.8 us
    all_to_all x1, blocking collectives, exchange(): return lax.all_to_all(array, AXES, split_axis=0, concat_axis=0, tiled=True)  16.9 us
    pallas_call x2, Pallas kernels, forward(): pl.pallas_call(forward_body, grid=(width // block,), in_specs=[pl.BlockSp...  10.7 us
    pallas_call x1, Pallas kernels, accumulate(): pl.pallas_call(functools.partial(accumulate_body, cap=cap), grid=(ngram,...  9.8 us
    pallas_call x1, Pallas kernels, lookup(): pl.pallas_call(functools.partial(lookup_body, cap=cap), grid=(ngram, widt...  9.17 us
  transfers between devices with their start and end apart: 25, of which 11 were waited for; matrix products, arithmetic and copies ran while one was open for 5% of the time, Pallas kernels for 8%

profile of v4, /device:TPU:50, one launch (start us, length us, event | category | flops | bytes accessed | tf_op | source)
XLA Modules:
  0.0 303.6 jit_solution(4423147534188554850)
XLA Ops:
  0.6 1.8 route.1
  2.5 16.9 %all_to_all.15 = s32[64,1,128]{2,1,0:T(1,128)} all-to-all(s32[64,1,128]{2,1,0:T(1,128)} %bitcast.39), channel_id=1, replica_groups=mesh['x'=4,'y'=4,'z'=4,'mp'=2] {'x','y','z'}, dimensions={0} | all-to-all | bytes 65536 | tf_op jit(solution)/shard_map/all_to_all | solution.py:249
  19.4 9.2 %lookup.1 = bf16[64,2,8,2048]{3,2,1,0:T(8,128)(2,1)} custom-call(s32[64,128]{1,0:T(8,128)} %bitcast.35, bf16[2,1024,2048]{2,1,0:T(8,128)(2,1)} %table_ref.1), custom_call_target="tpu_custom_call" | custom-call | tf_op jit(solution)/shard_map/lookup/pallas_call | solution.py:83
  28.5 9.3 %all-to-all-start.1 = ((bf16[64,2,8,2048]{3,2,1,0:T(8,128)(2,1)}), bf16[64,2,8,2048]{3,2,1,0:T(8,128)(2,1)}, u32[]{:S(2)}, u32[]{:S(2)}) async-start(bf16[64,2,8,2048]{3,2,1,0:T(8,128)(2,1)} %lookup.1), calls=%async_computation.1 | async-start | bytes 8388608 | tf_op jit(solution)/shard_map/all_to_all | solution.py:249
  37.9 0.6 collective-permute-start.5
  38.5 1.5 collective-permute-start.6
  40.0 1.2 collective-permute-start.7
  41.2 0.1 broadcast_in_dim.34
  41.4 46.8 %collective-permute-done.5 = bf16[64,2048]{1,0:T(8,128)(2,1)S(1)} collective-permute-done((bf16[64,2048]{1,0:T(8,128)(2,1)S(1)}, bf16[64,2048]{1,0:T(8,128)(2,1)S(1)}, u32[]{:S(2)}, u32[]{:S(2)}) %collective-permute-start.5) | collective-permute-done | bytes 262176 | tf_op jit(solution)/shard_map/ppermute | solution.py:264
  88.2 0.0 collective-permute-done.6
  88.2 3.5 %collective-permute-done.7 = bf16[64,2048]{1,0:T(8,128)(2,1)S(1)} collective-permute-done((bf16[64,2048]{1,0:T(8,128)(2,1)S(1)}, bf16[64,2048]{1,0:T(8,128)(2,1)S(1)}, u32[]{:S(2)}, u32[]{:S(2)}) %collective-permute-start.7) | collective-permute-done | bytes 262176 | tf_op jit(solution)/shard_map/ppermute | solution.py:264
  91.7 1.4 collective-permute-start.9
  93.1 0.7 collective-permute-start.8
  93.8 2.2 collective-permute-start.3
  96.0 2.2 collective-permute-start.4
  98.2 18.4 %collective-permute-done.9 = bf16[4,64,2048]{2,1,0:T(8,128)(2,1)S(1)} collective-permute-done((bf16[4,64,2048]{2,1,0:T(8,128)(2,1)S(1)}, bf16[4,64,2048]{2,1,0:T(8,128)(2,1)S(1)}, u32[]{:S(2)}, u32[]{:S(2)}) %collective-permute-start.9) | collective-permute-done | bytes 1048608 | tf_op jit(solution)/shard_map/ppermute | solution.py:268
  116.7 0.9 slice.9
  117.5 2.5 broadcast_in_dim.33
  120.1 1.1 bitcast_dynamic-update-slice_fusion.2
  121.1 0.0 collective-permute-done.8
  121.1 0.8 slice.8
  122.0 2.0 collective-permute-start.10
  124.0 1.1 bitcast_dynamic-update-slice_fusion.1
  125.1 4.8 %combine.1 = (bf16[8,256,256]{2,1,0:T(8,128)(2,1)}, f32[256,128]{1,0:T(8,128)}) custom-call(s32[2,256]{1,0:T(2,128)} %get-tuple-element.20.slot_ref, s32[1,256]{1,0:T(1,128)} %bitcast.41, bf16[64,2,8,2048]{3,2,1,0:T(8,128)(2,1)} %all-to-all-done.1.fetched_ref, bf16[256,2048]{1,0:T(8,128)(2,1)} %bytes_ref.1), custom_call_target="tpu_custom_call" | custom-call | tf_op jit(solution)/shard_map/combine/pallas_call | solution.py:139
  129.9 2.5 collective-permute-done.11
  132.4 0.0 collective-permute-start
  132.4 1.1 bitcast_dynamic-update-slice_fusion
  133.4 2.9 collective-permute-done.10
  136.4 2.3 fusion
  138.7 8.6 %product.1 = (bf16[256,1024]{1,0:T(8,128)(2,1)}, bf16[256,1024]{1,0:T(8,128)(2,1)}, bf16[256,1024]{1,0:T(8,128)(2,1)}, bf16[256,1024]{1,0:T(8,128)(2,1)}) custom-call(bf16[256,2048]{1,0:T(8,128)(2,1)} %refs_0_.1, bf16[256,2048]{1,0:T(8,128)(2,1)} %collective-permute-done.2.refs_1_, bf16[256,2048]{1,0:T(8,128)(2,1)} %collective-permute-done.3.refs_2_, ...), custom_call_target="tpu_custom_call" | custom-call | tf_op jit(solution)/shard_map/product/pallas_call | solution.py:291
  147.2 2.3 collective-permute-start.12
  149.6 2.5 collective-permute-start.13
  152.1 2.5 collective-permute-start.14
  154.6 0.0 collective-permute-start.1
  154.6 0.6 pad_add_fusion.place_ref
  155.2 7.0 %collective-permute-done.12.refs_1_ = bf16[256,1024]{1,0:T(8,128)(2,1)S(1)} collective-permute-done((bf16[256,1024]{1,0:T(8,128)(2,1)}, bf16[256,1024]{1,0:T(8,128)(2,1)S(1)}, u32[]{:S(2)}, u32[]{:S(2)}) %collective-permute-start.12) | collective-permute-done | bytes 524320 | tf_op jit(solution)/shard_map/ppermute | solution.py:264
  162.2 3.9 %collective-permute-done.14.refs_3_ = bf16[256,1024]{1,0:T(8,128)(2,1)S(1)} collective-permute-done((bf16[256,1024]{1,0:T(8,128)(2,1)}, bf16[256,1024]{1,0:T(8,128)(2,1)S(1)}, u32[]{:S(2)}, u32[]{:S(2)}) %collective-permute-start.14) | collective-permute-done | bytes 524320 | tf_op jit(solution)/shard_map/ppermute | solution.py:264
  166.1 0.0 copy-start.1
  166.1 0.8 copy-done.7
  166.9 0.0 copy-done.4
  166.9 0.3 copy-done.1
  167.3 5.1 %settle.1 = (bf16[8,256,256]{2,1,0:T(8,128)(2,1)}, bf16[8,256,256]{2,1,0:T(8,128)(2,1)}, f32[256,128]{1,0:T(8,128)}, bf16[256,1024]{1,0:T(8,128)(2,1)}, bf16[256...) custom-call(s32[2]{0:T(128)} %pad_add_fusion.place_ref, ...), custom_call_target="tpu_custom_call" | custom-call | tf_op jit(solution)/shard_map/settle/pallas_call | solution.py:362
  172.3 0.1 collective-permute-start.21
  172.4 0.5 collective-permute-start.22
  172.9 0.6 dynamic_slice.3
  173.5 1.9 collective-permute-done.22.in1_ref
  175.5 0.6 copy-done.11
  176.1 0.4 copy-done.2
  176.5 5.0 %dispatch.1 = bf16[64,2,8,2048]{3,2,1,0:T(8,128)(2,1)} custom-call(s32[2,256]{1,0:T(2,128)} %get-tuple-element.20.slot_ref, bf16[8,256,256]{2,1,0:T(8,128)(2,1)} %get-tuple-element.35.kept_ref, bf16[8,256,256]{2,1,0:T(8,128)(2,1)} %copy-done.2, f32[1,2048]{1,0:T(1,128)} %bitcast.38, bf16[8,256,256]{2,1,0:T(8,128)(2,1)} %get-tuple-element.22.own_ref.embedded_ref, ...), custom_call_target="tpu_custom_call" | custom-call | tf_op jit(solution)/shard_map/dispatch/pallas_call | solution.py:190
  181.5 11.4 %all-to-all-start.2 = ((bf16[64,2,8,2048]{3,2,1,0:T(8,128)(2,1)}), bf16[64,2,8,2048]{3,2,1,0:T(8,128)(2,1)}, u32[]{:S(2)}, u32[]{:S(2)}) async-start(bf16[64,2,8,2048]{3,2,1,0:T(8,128)(2,1)} %dispatch.1), calls=%async_computation.2 | async-start | bytes 8388608 | tf_op jit(solution)/shard_map/all_to_all | solution.py:249
  193.0 1.6 collective-permute-start.15
  194.7 0.5 collective-permute-start.16
  195.1 2.3 collective-permute-start.17
  197.4 50.5 %collective-permute-done.15.refs_1_ = bf16[256,1024]{1,0:T(8,128)(2,1)S(1)} collective-permute-done((bf16[256,1024]{1,0:T(8,128)(2,1)S(1)}, bf16[256,1024]{1,0:T(8,128)(2,1)S(1)}, u32[]{:S(2)}, u32[]{:S(2)}) %collective-permute-start.15) | collective-permute-done | bytes 524320 | tf_op jit(solution)/shard_map/ppermute | solution.py:264
  247.9 0.8 copy-done.8
  248.7 0.2 copy-done.9
  248.9 6.8 %forward.2 = (f32[256,2048]{1,0:T(8,128)}, bf16[256,2048]{1,0:T(8,128)(2,1)}, bf16[256,2048]{1,0:T(8,128)(2,1)}) custom-call(bf16[256,1024]{1,0:T(8,128)(2,1)} %get-tuple-element.28.refs_0_, bf16[256,1024]{1,0:T(8,128)(2,1)} %copy-done.8, bf16[256,1024]{1,0:T(8,128)(2,1)} %copy-done.9, bf16[1024,2048]{1,0:T(8,128)(2,1)} %bitcast.19.refs_4_.refs_3_.refs_1_), custom_call_target="tpu_custom_call" | custom-call | tf_op jit(solution)/shard_map/forward/pallas_call | solution.py:312
  255.7 9.0 %collective-permute-start.20 = (bf16[256,2048]{1,0:T(8,128)(2,1)}, bf16[256,2048]{1,0:T(8,128)(2,1)S(1)}, u32[]{:S(2)}, u32[]{:S(2)}) collective-permute-start(bf16[256,2048]{1,0:T(8,128)(2,1)} %get-tuple-element.34), channel_id=1, source_target_pairs={{0,32},{1,9},{8,40},{9,17},{16,48},{17,25},{24,56},{25,1},{32,64},... | collective-permute-start | bytes 3145736 | tf_op jit(solution)/shard_map/ppermute | solution.py:264
  264.6 3.9 %forward.3 = bf16[256,2048]{1,0:T(8,128)(2,1)} custom-call(bf16[256,1024]{1,0:T(8,128)(2,1)} %collective-permute-done.17.refs_0_, bf16[1024,2048]{1,0:T(8,128)(2,1)} %bitcast.19.refs_4_.refs_3_.refs_1_), custom_call_target="tpu_custom_call" | custom-call | tf_op jit(solution)/shard_map/forward/pallas_call | solution.py:312
  268.6 1.5 collective-permute-start.18
  270.1 18.4 %collective-permute-done.20 = bf16[256,2048]{1,0:T(8,128)(2,1)S(1)} collective-permute-done((bf16[256,2048]{1,0:T(8,128)(2,1)}, bf16[256,2048]{1,0:T(8,128)(2,1)S(1)}, u32[]{:S(2)}, u32[]{:S(2)}) %collective-permute-start.20) | collective-permute-done | bytes 1048608 | tf_op jit(solution)/shard_map/ppermute | solution.py:264
  288.5 2.5 collective-permute-done.19
  291.0 2.8 add_convert_fusion
  293.8 9.8 %accumulate.1 = bf16[2,1024,2048]{2,1,0:T(8,128)(2,1)} custom-call(s32[64,128]{1,0:T(8,128)} %bitcast.36, bf16[64,2,8,2048]{3,2,1,0:T(8,128)(2,1)} %all-to-all-done.2.arrived_ref), custom_call_target="tpu_custom_call" | custom-call | tf_op jit(solution)/shard_map/accumulate/pallas_call | solution.py:234
  (41 shorter events, 0.2 us)
Async XLA Ops:
  28.5 9.3 %copy-start.10 = (bf16[64,2048]{1,0:T(8,128)(2,1)S(1)}, bf16[64,2048]{1,0:T(8,128)(2,1)}, u32[]{:S(2)}) copy-start(bf16[64,2048]{1,0:T(8,128)(2,1)} %param.14) | copy-start | bytes 786436
  28.5 96.6 %all-to-all-start.1 = ((bf16[64,2,8,2048]{3,2,1,0:T(8,128)(2,1)}), bf16[64,2,8,2048]{3,2,1,0:T(8,128)(2,1)}, u32[]{:S(2)}, u32[]{:S(2)}) async-start(bf16[64,2,8,2048]{3,2,1,0:T(8,128)(2,1)} %lookup.1), calls=%async_computation.1 | async-start | bytes 8388608 | tf_op jit(solution)/shard_map/all_to_all | solution.py:249
  37.9 50.3 %collective-permute-start.5 = (bf16[64,2048]{1,0:T(8,128)(2,1)S(1)}, bf16[64,2048]{1,0:T(8,128)(2,1)S(1)}, u32[]{:S(2)}, u32[]{:S(2)}) collective-permute-start(bf16[64,2048]{1,0:T(8,128)(2,1)S(1)} %copy-done.10), channel_id=1, source_target_pairs={{0,24},{1,97},{8,0},{9,105},{16,8},{17,113},{24,16},{25,121},{32,5... | collective-permute-start | bytes 786440 | tf_op jit(solution)/shard_map/ppermute | solution.py:264
  38.5 49.7 %collective-permute-start.6 = (bf16[64,2048]{1,0:T(8,128)(2,1)S(1)}, bf16[64,2048]{1,0:T(8,128)(2,1)S(1)}, u32[]{:S(2)}, u32[]{:S(2)}) collective-permute-start(bf16[64,2048]{1,0:T(8,128)(2,1)S(1)} %copy-done.10), channel_id=1, source_target_pairs={{0,8},{1,33},{8,16},{9,41},{16,24},{17,49},{24,0},{25,57},{32,40},... | collective-permute-start | bytes 786440 | tf_op jit(solution)/shard_map/ppermute | solution.py:264
  40.0 51.7 %collective-permute-start.7 = (bf16[64,2048]{1,0:T(8,128)(2,1)S(1)}, bf16[64,2048]{1,0:T(8,128)(2,1)S(1)}, u32[]{:S(2)}, u32[]{:S(2)}) collective-permute-start(bf16[64,2048]{1,0:T(8,128)(2,1)S(1)} %copy-done.10), channel_id=1, source_target_pairs={{0,16},{1,65},{8,24},{9,73},{16,0},{17,81},{24,8},{25,89},{32,48},... | collective-permute-start | bytes 786440 | tf_op jit(solution)/shard_map/ppermute | solution.py:264
  91.7 25.0 %collective-permute-start.9 = (bf16[4,64,2048]{2,1,0:T(8,128)(2,1)S(1)}, bf16[4,64,2048]{2,1,0:T(8,128)(2,1)S(1)}, u32[]{:S(2)}, u32[]{:S(2)}) collective-permute-start(bf16[4,64,2048]{2,1,0:T(8,128)(2,1)S(1)} %bitcast_dynamic-update-slice_fusion.3), channel_id=1, source_target_pairs={{0,2},{2,4},{4,6},{6,0},{1,3},{3,5},{5,7},{7,1},{8,10},{10,12},{12... | collective-permute-start | bytes 3145736 | tf_op jit(solution)/shard_map/ppermute | solution.py:268
  93.1 28.0 %collective-permute-start.8 = (bf16[4,64,2048]{2,1,0:T(8,128)(2,1)S(1)}, bf16[4,64,2048]{2,1,0:T(8,128)(2,1)S(1)}, u32[]{:S(2)}, u32[]{:S(2)}) collective-permute-start(bf16[4,64,2048]{2,1,0:T(8,128)(2,1)S(1)} %bitcast_dynamic-update-slice_fusion.3), channel_id=1, source_target_pairs={{0,6},{2,0},{4,2},{6,4},{1,7},{3,1},{5,3},{7,5},{8,14},{10,8},{12,... | collective-permute-start | bytes 3145736 | tf_op jit(solution)/shard_map/ppermute | solution.py:268
  93.8 44.9 %collective-permute-start.2 = (bf16[256,2048]{1,0:T(8,128)(2,1)}, bf16[256,2048]{1,0:T(8,128)(2,1)}, u32[]{:S(2)}, u32[]{:S(2)}) collective-permute-start(bf16[256,2048]{1,0:T(8,128)(2,1)} %refs_0_.1), channel_id=1, source_target_pairs={{0,96},{1,25},{8,104},{9,1},{16,112},{17,9},{24,120},{25,17},{32,0... | collective-permute-start | bytes 3145736 | tf_op jit(solution)/shard_map/ppermute | solution.py:264
  93.8 44.9 %collective-permute-start.3 = (bf16[256,2048]{1,0:T(8,128)(2,1)}, bf16[256,2048]{1,0:T(8,128)(2,1)}, u32[]{:S(2)}, u32[]{:S(2)}) collective-permute-start(bf16[256,2048]{1,0:T(8,128)(2,1)} %refs_0_.1), channel_id=1, source_target_pairs={{0,64},{1,17},{8,72},{9,25},{16,80},{17,1},{24,88},{25,9},{32,96},... | collective-permute-start | bytes 3145736 | tf_op jit(solution)/shard_map/ppermute | solution.py:264
  96.0 42.6 %collective-permute-start.4 = (bf16[256,2048]{1,0:T(8,128)(2,1)}, bf16[256,2048]{1,0:T(8,128)(2,1)}, u32[]{:S(2)}, u32[]{:S(2)}) collective-permute-start(bf16[256,2048]{1,0:T(8,128)(2,1)} %refs_0_.1), channel_id=1, source_target_pairs={{0,32},{1,9},{8,40},{9,17},{16,48},{17,25},{24,56},{25,1},{32,64},... | collective-permute-start | bytes 3145736 | tf_op jit(solution)/shard_map/ppermute | solution.py:264
  117.5 14.8 %collective-permute-start.11 = (bf16[2,64,2048]{2,1,0:T(8,128)(2,1)}, bf16[2,64,2048]{2,1,0:T(8,128)(2,1)}, u32[]{:S(2)}, u32[]{:S(2)}) collective-permute-start(bf16[2,64,2048]{2,1,0:T(8,128)(2,1)} %slice.9), channel_id=1, source_target_pairs={{0,2},{2,4},{4,6},{6,0},{1,3},{3,5},{5,7},{7,1},{8,10},{10,12},{12... | collective-permute-start | bytes 1572872 | tf_op jit(solution)/shard_map/ppermute | solution.py:268
  122.0 14.4 %collective-permute-start.10 = (bf16[2,64,2048]{2,1,0:T(8,128)(2,1)}, bf16[2,64,2048]{2,1,0:T(8,128)(2,1)}, u32[]{:S(2)}, u32[]{:S(2)}) collective-permute-start(bf16[2,64,2048]{2,1,0:T(8,128)(2,1)} %slice.8), channel_id=1, source_target_pairs={{0,6},{2,0},{4,2},{6,4},{1,7},{3,1},{5,3},{7,5},{8,14},{10,8},{12,... | collective-permute-start | bytes 1572872 | tf_op jit(solution)/shard_map/ppermute | solution.py:268
  132.4 33.7 %collective-permute-start = (bf16[8,256,256]{2,1,0:T(8,128)(2,1)}, bf16[8,256,256]{2,1,0:T(8,128)(2,1)S(1)}, u32[]{:S(2)}, u32[]{:S(2)}) collective-permute-start(bf16[8,256,256]{2,1,0:T(8,128)(2,1)} %get-tuple-element.22.own_ref.embedded_ref), channel_id=1, source_target_pairs={{0,1},{1,0},{2,3},{3,2},{4,5},{5,4},{6,7},{7,6},{8,9},{9,8},{10,11... | collective-permute-start | bytes 3145736 | tf_op jit(solution)/shard_map/ppermute | solution.py:253
  138.7 15.9 %copy-start.3 = (f32[256,128]{1,0:T(8,128)S(1)}, f32[256,128]{1,0:T(8,128)}, u32[]{:S(2)}) copy-start(f32[256,128]{1,0:T(8,128)} %get-tuple-element.23.mine_ref.sq0_ref) | copy-start | bytes 393220
  147.2 25.7 %copy-start.12 = (f32[4096]{0:T(1024)S(1)}, f32[4096]{0:T(1024)}, u32[]{:S(2)}) copy-start(f32[4096]{0:T(1024)} %param.13) | copy-start | bytes 49156
  147.2 15.0 %collective-permute-start.12 = (bf16[256,1024]{1,0:T(8,128)(2,1)}, bf16[256,1024]{1,0:T(8,128)(2,1)S(1)}, u32[]{:S(2)}, u32[]{:S(2)}) collective-permute-start(bf16[256,1024]{1,0:T(8,128)(2,1)} %get-tuple-element.25), channel_id=1, source_target_pairs={{0,32},{1,9},{8,40},{9,17},{16,48},{17,25},{24,56},{25,1},{32,64},... | collective-permute-start | bytes 1572872 | tf_op jit(solution)/shard_map/ppermute | solution.py:264
  149.6 12.6 %collective-permute-start.13 = (bf16[256,1024]{1,0:T(8,128)(2,1)}, bf16[256,1024]{1,0:T(8,128)(2,1)S(1)}, u32[]{:S(2)}, u32[]{:S(2)}) collective-permute-start(bf16[256,1024]{1,0:T(8,128)(2,1)} %get-tuple-element.26), channel_id=1, source_target_pairs={{0,64},{1,17},{8,72},{9,25},{16,80},{17,1},{24,88},{25,9},{32,96},... | collective-permute-start | bytes 1572872 | tf_op jit(solution)/shard_map/ppermute | solution.py:264
  152.1 14.0 %collective-permute-start.14 = (bf16[256,1024]{1,0:T(8,128)(2,1)}, bf16[256,1024]{1,0:T(8,128)(2,1)S(1)}, u32[]{:S(2)}, u32[]{:S(2)}) collective-permute-start(bf16[256,1024]{1,0:T(8,128)(2,1)} %get-tuple-element.27), channel_id=1, source_target_pairs={{0,96},{1,25},{8,104},{9,1},{16,112},{17,9},{24,120},{25,17},{32,0... | collective-permute-start | bytes 1572872 | tf_op jit(solution)/shard_map/ppermute | solution.py:264
  154.6 11.5 %collective-permute-start.1 = (f32[256,128]{1,0:T(8,128)S(1)}, f32[256,128]{1,0:T(8,128)S(1)}, u32[]{:S(2)}, u32[]{:S(2)}) collective-permute-start(f32[256,128]{1,0:T(8,128)S(1)} %copy-done.3), channel_id=1, source_target_pairs={{0,1},{1,0},{2,3},{3,2},{4,5},{5,4},{6,7},{7,6},{8,9},{9,8},{10,11... | collective-permute-start | bytes 393224 | tf_op jit(solution)/shard_map/ppermute | solution.py:253
  162.2 3.9 %copy-start.5 = (bf16[256,1024]{1,0:T(8,128)(2,1)}, bf16[256,1024]{1,0:T(8,128)(2,1)S(1)}, u32[]{:S(2)}) copy-start(bf16[256,1024]{1,0:T(8,128)(2,1)S(1)} %collective-permute-done.12.refs_1_) | copy-start | bytes 1572868
  162.2 3.9 %copy-start.6 = (bf16[256,1024]{1,0:T(8,128)(2,1)}, bf16[256,1024]{1,0:T(8,128)(2,1)S(1)}, u32[]{:S(2)}) copy-start(bf16[256,1024]{1,0:T(8,128)(2,1)S(1)} %collective-permute-done.13.refs_2_) | copy-start | bytes 1572868
  166.1 0.8 copy-start.7
  166.1 0.8 copy-start.4
  166.1 1.2 copy-start.1
  172.3 3.1 %collective-permute-start.21 = (bf16[8,256,256]{2,1,0:T(8,128)(2,1)}, bf16[8,256,256]{2,1,0:T(8,128)(2,1)S(1)}, u32[]{:S(2)}, u32[]{:S(2)}) collective-permute-start(bf16[8,256,256]{2,1,0:T(8,128)(2,1)} %get-tuple-element.36), channel_id=1, source_target_pairs={{0,1},{1,0},{2,3},{3,2},{4,5},{5,4},{6,7},{7,6},{8,9},{9,8},{10,11... | collective-permute-start | bytes 3145736 | tf_op jit(solution)/shard_map/ppermute | solution.py:253
  172.4 3.0 %collective-permute-start.22 = (f32[256,128]{1,0:T(8,128)}, f32[256,128]{1,0:T(8,128)S(1)}, u32[]{:S(2)}, u32[]{:S(2)}) collective-permute-start(f32[256,128]{1,0:T(8,128)} %get-tuple-element.37.in0_ref), channel_id=1, source_target_pairs={{0,1},{1,0},{2,3},{3,2},{4,5},{5,4},{6,7},{7,6},{8,9},{9,8},{10,11... | collective-permute-start | bytes 393224 | tf_op jit(solution)/shard_map/ppermute | solution.py:253
  175.5 0.6 copy-start.11
  175.5 1.0 copy-start.2
  181.5 11.5 %copy-start.14 = (bf16[256,1024]{1,0:T(8,128)(2,1)S(1)}, bf16[256,1024]{1,0:T(8,128)(2,1)}, u32[]{:S(2)}) copy-start(bf16[256,1024]{1,0:T(8,128)(2,1)} %get-tuple-element.29) | copy-start | bytes 1572868
  181.5 13.1 %copy-start.13 = (bf16[256,1024]{1,0:T(8,128)(2,1)S(1)}, bf16[256,1024]{1,0:T(8,128)(2,1)}, u32[]{:S(2)}) copy-start(bf16[256,1024]{1,0:T(8,128)(2,1)} %get-tuple-element.30) | copy-start | bytes 1572868
  181.5 112.3 %all-to-all-start.2 = ((bf16[64,2,8,2048]{3,2,1,0:T(8,128)(2,1)}), bf16[64,2,8,2048]{3,2,1,0:T(8,128)(2,1)}, u32[]{:S(2)}, u32[]{:S(2)}) async-start(bf16[64,2,8,2048]{3,2,1,0:T(8,128)(2,1)} %dispatch.1), calls=%async_computation.2 | async-start | bytes 8388608 | tf_op jit(solution)/shard_map/all_to_all | solution.py:249
  193.0 54.9 %collective-permute-start.15 = (bf16[256,1024]{1,0:T(8,128)(2,1)S(1)}, bf16[256,1024]{1,0:T(8,128)(2,1)S(1)}, u32[]{:S(2)}, u32[]{:S(2)}) collective-permute-start(bf16[256,1024]{1,0:T(8,128)(2,1)S(1)} %copy-done.14), channel_id=1, source_target_pairs={{0,32},{1,9},{8,40},{9,17},{16,48},{17,25},{24,56},{25,1},{32,64},... | collective-permute-start | bytes 1572872 | tf_op jit(solution)/shard_map/ppermute | solution.py:264
  194.7 53.2 %collective-permute-start.16 = (bf16[256,1024]{1,0:T(8,128)(2,1)S(1)}, bf16[256,1024]{1,0:T(8,128)(2,1)S(1)}, u32[]{:S(2)}, u32[]{:S(2)}) collective-permute-start(bf16[256,1024]{1,0:T(8,128)(2,1)S(1)} %copy-done.13), channel_id=1, source_target_pairs={{0,96},{1,25},{8,104},{9,1},{16,112},{17,9},{24,120},{25,17},{32,0... | collective-permute-start | bytes 1572872 | tf_op jit(solution)/shard_map/ppermute | solution.py:264
  195.1 69.5 %collective-permute-start.17 = (bf16[256,1024]{1,0:T(8,128)(2,1)}, bf16[256,1024]{1,0:T(8,128)(2,1)}, u32[]{:S(2)}, u32[]{:S(2)}) collective-permute-start(bf16[256,1024]{1,0:T(8,128)(2,1)} %get-tuple-element.32), channel_id=1, source_target_pairs={{0,64},{1,17},{8,72},{9,25},{16,80},{17,1},{24,88},{25,9},{32,96},... | collective-permute-start | bytes 1572872 | tf_op jit(solution)/shard_map/ppermute | solution.py:264
  247.9 0.8 copy-start.8
  247.9 1.0 copy-start.9
  255.7 35.3 %copy-start = (f32[256,2048]{1,0:T(8,128)S(1)}, f32[256,2048]{1,0:T(8,128)}, u32[]{:S(2)}) copy-start(f32[256,2048]{1,0:T(8,128)} %get-tuple-element.31) | copy-start | bytes 6291460
  255.7 32.8 %collective-permute-start.20 = (bf16[256,2048]{1,0:T(8,128)(2,1)}, bf16[256,2048]{1,0:T(8,128)(2,1)S(1)}, u32[]{:S(2)}, u32[]{:S(2)}) collective-permute-start(bf16[256,2048]{1,0:T(8,128)(2,1)} %get-tuple-element.34), channel_id=1, source_target_pairs={{0,32},{1,9},{8,40},{9,17},{16,48},{17,25},{24,56},{25,1},{32,64},... | collective-permute-start | bytes 3145736 | tf_op jit(solution)/shard_map/ppermute | solution.py:264
  264.6 26.4 %collective-permute-start.19 = (bf16[256,2048]{1,0:T(8,128)(2,1)}, bf16[256,2048]{1,0:T(8,128)(2,1)}, u32[]{:S(2)}, u32[]{:S(2)}) collective-permute-start(bf16[256,2048]{1,0:T(8,128)(2,1)} %get-tuple-element.33), channel_id=1, source_target_pairs={{0,96},{1,25},{8,104},{9,1},{16,112},{17,9},{24,120},{25,17},{32,0... | collective-permute-start | bytes 3145736 | tf_op jit(solution)/shard_map/ppermute | solution.py:264
  268.6 22.4 %collective-permute-start.18 = (bf16[256,2048]{1,0:T(8,128)(2,1)}, bf16[256,2048]{1,0:T(8,128)(2,1)S(1)}, u32[]{:S(2)}, u32[]{:S(2)}) collective-permute-start(bf16[256,2048]{1,0:T(8,128)(2,1)} %forward.3), channel_id=1, source_target_pairs={{0,64},{1,17},{8,72},{9,25},{16,80},{17,1},{24,88},{25,9},{32,96},... | collective-permute-start | bytes 3145736 | tf_op jit(solution)/shard_map/ppermute | solution.py:264
